TPU v7x, 128 devices: a whole 4x4x4 slice. The times are simulated.
128 devices in a mesh: ens: 64 (over z, y, x_hi, core), batch: 2 (over x_lo).
Axes of the slice: x: 4 (x_hi: 2, x_lo: 2; x = x_hi * 2 + x_lo), y: 4, z: 4, core: 2. Of those that a mesh axis runs over, the one named last changes fastest.
Arguments:
- replay_obs: bfloat16 [512, 1024], P('batch'), may hold values from -4.1875 to 4.1875
- replay_next: bfloat16 [512, 1024], P('batch'), may hold values from -4.1875 to 4.1875
- batch_rows: int32 [64], P('batch'), may hold values from 0 to 255
- data_action: int32 [64], P('batch'), may hold values from 0 to 255
- next_action: int32 [64], P('batch'), may hold values from 0 to 255
- sampled_actions: int32 [64, 16], P('batch'), may hold values from 0 to 255
- reward: float32 [64], P('batch'), may hold values from -6 to 6
- next_logp: float32 [64], P('batch'), may hold values from -6 to 2
- action_table: bfloat16 [256, 1024], replicated, may hold values from -4.1875 to 4.1875
- w1: bfloat16 [64, 4096, 1024], P('ens'), may hold values from -0.1875 to 0.1875
- w2: float32 [64, 4096], P('ens'), may hold values from -0.375 to 0.375
Outputs:
- grad_w1: float32 [64, 4096, 1024], P('ens', 'batch')
- grad_w2: float32 [64, 4096], P('ens')
- critic_stats: float32 [64, 3], P('ens')
Inputs may be any that keep to these rules, and one draw needn't show every extreme that they name: `batch_rows`: each entry is a row of the own block of 256 replay rows that holds its state.
All inputs are finite; a program needn't handle non-finite values.
Results may differ from a plain program's by a relative error of at most 0.0045.
Values may be sent and summed in bfloat16 or wider, within the bound.
A program may use at most 128 MiB of HBM per device.

v0:
```python
from functools import reduce

import jax
import jax.numpy as jnp
from jax import lax
from jax.sharding import Mesh
from jax.sharding import PartitionSpec as P

ENS = ("ens_0", "ens_1", "ens_2", "ens_3")


discount = 0.99
entropy_temp = 0.2
penalty_weight = 1.0
diversity_weight = 1000.0


def side_by_side(arrays, axis, dim, along):
    ends, at = ([], 0)
    for a in arrays[:-1]:
        at += a.shape[along]
        ends.append(at)
    both = jnp.concatenate(arrays, axis=along)
    return tuple(jnp.split(lax.all_gather(both, axis, axis=dim, tiled=True), ends, axis=along))


def copy_for_each(x, axis):
    count = lax.axis_size(axis)
    return lax.all_to_all(jnp.broadcast_to(x[None], (count, *x.shape)), axis, 0, 0, tiled=True)


def taken_together(x, axis):
    return copy_for_each(x, axis).sum(axis=0)


def together(arrays, axis):
    ends = [0]
    for a in arrays:
        ends.append(ends[-1] + a.size)
    subtotal = taken_together(jnp.concatenate([a.ravel() for a in arrays]), axis)
    return tuple((subtotal[b:e].reshape(a.shape) for a, b, e in zip(arrays, ends, ends[1:])))


def combined_by_axis(x, axes, combine):
    for axis in axes:
        pieces = jax.tree.map(lambda part: lax.all_gather(part, axis), x)
        x = jax.tree.map(lambda part: part[0], pieces)
        for k in range(1, lax.axis_size(axis)):
            x = combine(x, jax.tree.map(lambda part: part[k], pieces))
    return x


def silu_terms(preact):
    sigmoid_v = jax.nn.sigmoid(preact)
    silu_out = preact * sigmoid_v
    slope_one = sigmoid_v * (1.0 + preact * (1.0 - sigmoid_v))
    return (silu_out, slope_one, sigmoid_v)


def embed_rows(index_arr, action_table):
    one_hot = (index_arr[..., None] == jnp.arange(action_table.shape[0], dtype=jnp.int32)).astype(
        jnp.bfloat16
    )
    return jnp.dot(one_hot, action_table, preferred_element_type=jnp.float32)


def join_parts(left_pair, right_pair):
    return (left_pair[0] + right_pair[0], jnp.minimum(left_pair[1], right_pair[1]))


def forward_critic(rows_all, weight, readout, data_lo, data_hi):
    preact = jnp.dot(rows_all, weight.T, preferred_element_type=jnp.float32)
    silu_out, slope_one, sigmoid_v = silu_terms(preact)
    q_vals = jnp.sum(silu_out * readout, axis=-1)
    coeffs = (readout * slope_one[data_lo:data_hi]).astype(jnp.bfloat16)
    grad_in = jnp.dot(coeffs, weight, preferred_element_type=jnp.float32)
    return [preact, silu_out, slope_one, sigmoid_v, q_vals, coeffs, grad_in]


def body(
    replay_obs,
    replay_next,
    batch_rows,
    data_action,
    next_action,
    sampled_actions,
    reward,
    next_logp,
    action_table,
    w1,
    w2,
):
    per_dev = batch_rows.shape[0]
    samples = sampled_actions.shape[1]
    critics = w1.shape[0]
    width = replay_obs.shape[1]
    hidden_total = w1.shape[1]
    batch_count = lax.axis_size("batch")
    states_total = per_dev * batch_count
    critics_total = critics * lax.axis_size(ENS)
    obs_rows = jnp.take(replay_obs, batch_rows, axis=0).astype(jnp.float32)
    next_rows = jnp.take(replay_next, batch_rows, axis=0).astype(jnp.float32)
    x_next = (next_rows + embed_rows(next_action, action_table)).astype(jnp.bfloat16)
    x_data = (obs_rows + embed_rows(data_action, action_table)).astype(jnp.bfloat16)
    x_samp = (obs_rows[:, None, :] + embed_rows(sampled_actions, action_table)).astype(jnp.bfloat16)
    x_samp = x_samp.reshape(per_dev * samples, width)
    h_count = hidden_total // batch_count
    h_start = lax.axis_index("batch") * h_count
    stat_lo = lax.axis_index("batch") * per_dev
    all_next, all_data, all_samp = (
        *side_by_side((x_next, x_data), "batch", 0, 1),
        lax.all_gather(x_samp, "batch", axis=0, tiled=True),
    )
    rows_all = jnp.concatenate([all_next, all_data, all_samp], axis=0)
    weights = [lax.dynamic_slice_in_dim(w1[0], h_start, h_count, 0)]
    readouts = [lax.dynamic_slice_in_dim(w2[0], h_start, h_count, 0)]
    saved = [forward_critic(rows_all, weights[0], readouts[0], states_total, 2 * states_total)]
    owner = jnp.arange(states_total, dtype=jnp.int32) // per_dev == lax.axis_index("batch")
    reward_own = jnp.where(owner, jnp.tile(reward, batch_count), 0.0)
    logp_own = jnp.where(owner, jnp.tile(next_logp, batch_count), 0.0)
    q_sums, grad_sums, reward_all, logp_all = together(
        (
            jnp.stack([entry[4] for entry in saved]),
            jnp.stack([entry[6] for entry in saved]),
            reward_own,
            logp_own,
        ),
        "batch",
    )
    critic = 0
    saved[critic][4] = q_sums[critic]
    saved[critic][6] = grad_sums[critic]
    x_back = rows_all[states_total:]
    data_hi = 2 * states_total
    critic = 0
    grad_in = saved[critic][6]
    in_norm = jnp.sqrt(jnp.sum(grad_in * grad_in, axis=-1, keepdims=True) + 1.0)
    norms = [in_norm]
    units = [grad_in / in_norm]
    local_floor = reduce(jnp.minimum, [entry[4][:states_total] for entry in saved])
    local_spread = reduce(jnp.add, units)
    spread, target_floor = combined_by_axis((local_spread, local_floor), ENS, join_parts)
    target = reward_all + discount * (target_floor - entropy_temp * logp_all)
    critic = 0
    preact, silu_out, slope_one, sigmoid_v, q_vals, coeffs, grad_in = saved[critic]
    in_norm = norms[critic]
    unit_dir = units[critic]
    weight = weights[critic]
    readout = readouts[critic]
    q_data = q_vals[states_total:data_hi]
    q_samp = q_vals[data_hi:].reshape(states_total, samples)
    pre_data = preact[states_total:data_hi]
    sig_data = sigmoid_v[states_total:data_hi]
    slope_data = slope_one[states_total:data_hi]
    slope_samp = slope_one[data_hi:]
    td_gap = q_data - target
    log_mass = jnp.log(jnp.sum(jnp.exp(q_samp), axis=-1))
    action_prob = jnp.exp(q_samp - log_mass[:, None])
    div_row = jnp.sum(unit_dir * (spread - unit_dir), axis=-1)
    row_stats = jnp.stack([td_gap * td_gap, log_mass - q_data, div_row])
    own_stats = lax.dynamic_slice_in_dim(row_stats, stat_lo, per_dev, 1)
    stat_list = [jnp.sum(own_stats, axis=1)]
    dq_data = (2.0 * td_gap - penalty_weight) / states_total
    dq_samp = (penalty_weight * action_prob / states_total).reshape(states_total * samples)
    dunit = 2.0 * diversity_weight / (critics_total - 1) / states_total * (spread - unit_dir)
    dgrad = (
        (dunit - unit_dir * jnp.sum(unit_dir * dunit, axis=-1, keepdims=True)) / in_norm
    ).astype(jnp.bfloat16)
    dcoef = jnp.dot(dgrad, weight.T, preferred_element_type=jnp.float32)
    curve_two = sig_data * (1.0 - sig_data) * (2.0 + pre_data * (1.0 - 2.0 * sig_data))
    dpre_data = (dq_data[:, None] * readout * slope_data + dcoef * readout * curve_two).astype(
        jnp.bfloat16
    )
    dpre_samp = (dq_samp[:, None] * readout * slope_samp).astype(jnp.bfloat16)
    grad_v = jnp.sum(dq_data[:, None] * silu_out[states_total:data_hi], axis=0)
    grad_v = grad_v + jnp.sum(dq_samp[:, None] * silu_out[data_hi:], axis=0)
    grad_v = grad_v + jnp.sum(dcoef * slope_data, axis=0)
    readout_grads = [
        lax.dynamic_update_slice_in_dim(jnp.zeros((hidden_total,), jnp.float32), grad_v, h_start, 0)
    ]
    dpre_list = jnp.concatenate([dpre_data, dpre_samp], axis=0)
    totals = (
        taken_together(jnp.stack(stat_list), "batch"),
        taken_together(jnp.stack(readout_grads), "batch"),
    )
    critic_stats = totals[0] / states_total
    grad_w2 = totals[1]
    grad_w1 = jnp.stack(
        [
            jnp.dot(dpre_list.T, x_back, preferred_element_type=jnp.float32)
            + jnp.dot(coeffs.T, dgrad, preferred_element_type=jnp.float32)
        ]
    )
    return (grad_w1, grad_w2, critic_stats)


def solution(mesh):
    finer = Mesh(
        mesh.devices.reshape(4, 4, 2, 2, mesh.shape["batch"]),
        ("ens_0", "ens_1", "ens_2", "ens_3", "batch"),
    )
    placed = (
        P("batch", None),
        P("batch", None),
        P("batch"),
        P("batch"),
        P("batch"),
        P("batch", None),
        P("batch"),
        P("batch"),
        P(),
        P(ENS, None, None),
        P(ENS, None),
    )
    return jax.shard_map(
        body,
        mesh=finer,
        in_specs=placed,
        out_specs=(P(ENS, "batch", None), P(ENS, None), P(ENS, None)),
        check_vma=False,
    )
```

profile of v0, /device:TPU:0, one launch (start us, length us, event | category | flops | bytes accessed | tf_op | source)
XLA Modules:
  0.0 188.1 jit_solution(1777028769227150099)
XLA Ops:
  7.2 0.7 compare_and_fusion
  8.6 0.8 copy.18
  9.4 1.8 gather_fusion.1
  11.3 1.5 add_convert_fusion
  14.3 1.8 gather_fusion
  16.1 0.9 fusion.27
  17.0 0.9 fusion.26
  17.9 5.8 %all_gather.40 = bf16[64,2048]{1,0:T(8,128)(2,1)S(1)} all-gather(bf16[32,2048]{1,0:T(8,128)(2,1)S(1)} %pad_maximum_fusion), channel_id=1, replica_groups=mesh['ens_0'=4,'ens_1'=4,'ens_2'=2,'ens_3'=2,'batch'=2] {'batch'}, dimensions={0}, use_global_device_ids=true | all-gather | bytes 393216 | tf_op jit(solution)/shard_map/all_gather | solution.py:24
  23.6 0.7 constant_dynamic-slice_fusion
  24.4 26.6 %all-gather.8.cloned.1.call-done = bf16[1024,1024]{1,0:T(8,128)(2,1)} async-done(((bf16[512,1024]{1,0:T(8,128)(2,1)}), bf16[1024,1024]{1,0:T(8,128)(2,1)}) %all-gather.8.cloned.1.call-update) | async-done | bytes 2097168 | tf_op jit(solution)/shard_map/all_gather | solution.py:112
  51.0 18.1 %add_divide_fusion = (f32[1152,2048]{1,0:T(8,128)}, f32[1152,2048]{1,0:T(8,128)}, f32[1152]{0:T(1024)S(1)}, f32[1152,2048]{1,0:T(8,128)}, f32[1152,2048]{1,0:T(8,128)}) fusion(f32[2048]{0:T(1024)S(1)} %bitcast.62, bf16[1,4096,1024]{2,1,0:T(8,128)(2,1)} %param.22, s32[]{:T(128)S(6)} %select_n.27, bf16[1024,1024]{1,0:T(8,128)(2,1)} %all-gather.8.cloned.1.call-done, ...), kind=kOutput, calls=%fused_computation.4 | convolution fusion | flops 4862508032 | bytes 44315140 | tf_op jit(solution)/shard_map/dot_general | solution.py:72
  69.1 3.2 %fusion.23 = f32[8,8,8,128]{3,2,1,0:T(8,128)S(1)} fusion(bf16[1,4096,1024]{2,1,0:T(8,128)(2,1)} %param.22, s32[]{:T(128)S(6)} %select_n.27, f32[1152,2048]{1,0:T(8,128)} %get-tuple-element.14, f32[2048]{0:T(1024)S(1)} %bitcast.63), kind=kOutput, calls=%fused_computation.32 | convolution fusion | flops 268697600 | bytes 4988932 | tf_op jit(solution)/shard_map/dot_general | solution.py:76
  72.4 1.2 concatenate.17
  73.9 10.6 %all_to_all.16 = f32[2,1,66816]{2,1,0:T(1,128)S(1)} all-to-all(f32[2,1,66816]{2,1,0:T(1,128)S(1)} %broadcast_in_dim.23), channel_id=1, replica_groups=mesh['ens_0'=4,'ens_1'=4,'ens_2'=2,'ens_3'=2,'batch'=2] {'batch'}, dimensions={0} | all-to-all | bytes 1069056 | tf_op jit(solution)/shard_map/all_to_all | solution.py:29
  84.4 0.8 reduce_sum.111
  85.5 0.8 broadcast_divide_fusion.1
  87.9 10.7 %all-reduce = f32[256]{0:T(256)S(1)} all-reduce(f32[256]{0:T(256)S(1)} %get-tuple-element.18), channel_id=2, replica_groups=mesh['ens_0'=4,'ens_1'=4,'ens_2'=2,'ens_3'=2,'batch'=2] {'ens_0'}, use_global_device_ids=true, to_apply=%add | all-reduce | flops 256 | bytes 2048
  98.6 9.7 %all-gather.1 = f32[4,1,64]{2,1,0:T(1,128)S(1)} all-gather(f32[1,1,64]{2,1,0:T(1,128)S(1)} %minimum_bitcast_fusion), channel_id=1, replica_groups=mesh['ens_0'=4,'ens_1'=4,'ens_2'=2,'ens_3'=2,'batch'=2] {'ens_1'}, dimensions={0}, use_global_device_ids=true | all-gather | bytes 1280 | tf_op jit(solution)/shard_map/all_gather | solution.py:46
  108.3 5.7 %all-gather.2 = f32[2,1,64]{2,1,0:T(1,128)S(1)} all-gather(f32[1,1,64]{2,1,0:T(1,128)S(1)} %slice_minimum_fusion.2), channel_id=1, replica_groups=mesh['ens_0'=4,'ens_1'=4,'ens_2'=2,'ens_3'=2,'batch'=2] {'ens_2'}, dimensions={0}, use_global_device_ids=true | all-gather | bytes 768 | tf_op jit(solution)/shard_map/all_gather | solution.py:46
  114.1 1.9 %slice_add_fusion.5 = f32[1,64,1024]{2,1,0:T(8,128)} fusion(f32[4,64,1024]{2,1,0:T(8,128)} %all-gather.10.cloned.1.call-done), kind=kLoop, calls=%fused_computation.55 | loop fusion | flops 196608 | bytes 1310720 | tf_op jit(solution)/shard_map/add | solution.py:68
  116.2 1.8 all-gather.3
  118.1 9.1 %fusion = (f32[2048]{0:T(1024)S(1)}, bf16[1024,2048]{1,0:T(8,128)(2,1)}) fusion(f32[1152,2048]{1,0:T(8,128)} %get-tuple-element.16, f32[1024]{0:T(1024)S(1)} %exponential_multiply_fusion, f32[1152,2048]{1,0:T(8,128)} %get-tuple-element.14, f32[2048]{0:T(1024)S(1)} %bitcast.64), kind=kLoop, calls=%fused_computation.6 | loop fusion | flops 10483712 | bytes 20992000 | tf_op jit(solution)/shard_map/reduce_sum | solution.py:176
  127.2 11.1 %all-gather.12.cloned.1.call-done = f32[4,64,1024]{2,1,0:T(8,128)} async-done(((f32[1,64,1024]{2,1,0:T(8,128)}), f32[4,64,1024]{2,1,0:T(8,128)}) %all-gather.12.cloned.1.call-update) | async-done | bytes 1048592 | tf_op jit(solution)/shard_map/all_gather | solution.py:46
  138.3 1.2 slice_add_fusion.2
  139.5 8.5 %all_gather.49 = f32[2,64,1024]{2,1,0:T(8,128)S(1)} all-gather(f32[1,64,1024]{2,1,0:T(8,128)S(1)} %slice_add_fusion.2), channel_id=1, replica_groups=mesh['ens_0'=4,'ens_1'=4,'ens_2'=2,'ens_3'=2,'batch'=2] {'ens_2'}, dimensions={0}, use_global_device_ids=true | all-gather | bytes 786432 | tf_op jit(solution)/shard_map/all_gather | solution.py:46
  148.1 2.2 %all_gather.50 = f32[2,64,1024]{2,1,0:T(8,128)S(1)} all-gather(f32[1,64,1024]{2,1,0:T(8,128)S(1)} %slice_add_fusion.1), channel_id=1, replica_groups=mesh['ens_0'=4,'ens_1'=4,'ens_2'=2,'ens_3'=2,'batch'=2] {'ens_3'}, dimensions={0}, use_global_device_ids=true | all-gather | bytes 786432 | tf_op jit(solution)/shard_map/all_gather | solution.py:46
  151.3 3.4 %all-to-all-start.2 = ((f32[2,1,3]{2,1,0:T(1,128)}), f32[2,1,3]{2,1,0:T(1,128)S(1)}, u32[]{:S(2)}, u32[]{:S(2)}) async-start(f32[2,1,3]{2,1,0:T(1,128)} %broadcast_in_dim.26), calls=%async_computation.2 | async-start | bytes 2048 | tf_op jit(solution)/shard_map/all_to_all | solution.py:29
  154.7 4.3 %multiply_reduce_fusion.1 = (f32[2048]{0:T(1024)S(1)}, bf16[64,2048]{1,0:T(8,128)(2,1)S(1)}, f32[2048]{0:T(1024)S(1)}) fusion(f32[1152,2048]{1,0:T(8,128)} %get-tuple-element.14, f32[1152,2048]{1,0:T(8,128)} %get-tuple-element.25, f32[1152,2048]{1,0:T(8,128)} %get-tuple-element.13, f32[2048]{0:T(1024)S(1)} %bitcast.65, f32[64]{0:T(128)S(1)} %add_multiply_fusion.1, ...), kind=kOutput, calls=%fused_computation.47 | convolution fusion | flops 271118336 | bytes 7103236 | tf_op jit(solution)/shard_map/dot_general | solution.py:169
  159.0 8.3 %fusion.2 = f32[2048,1024]{1,0:T(8,128)S(1)} fusion(bf16[1024,2048]{1,0:T(8,128)(2,1)} %get-tuple-element.22, bf16[64,2048]{1,0:T(8,128)(2,1)S(1)} %get-tuple-element.12, bf16[1024,1024]{1,0:T(8,128)(2,1)} %all-gather.8.cloned.1.call-done, bf16[64,1024]{1,0:T(8,128)(2,1)S(1)} %get-tuple-element.20), kind=kOutput, calls=%fused_computation.10 | convolution fusion | flops 4576772096 | bytes 15073280 | tf_op jit(solution)/shard_map/dot_general | solution.py:190
  167.3 5.8 %add_bitcast_fusion = f32[1,2048,1024]{2,1,0:T(8,128)} fusion(f32[2048,1024]{1,0:T(8,128)S(1)} %fusion.2, f32[1,64,1024]{2,1,0:T(8,128)S(1)} %get-tuple-element.8, f32[64]{0:T(128)S(1)} %get-tuple-element.5, f32[64]{0:T(128)S(1)} %add_sqrt_fusion, f32[1152,2048]{1,0:T(8,128)} %get-tuple-element.14, f32[2048]{0:T(1024)S(1)} %bitcast.66, ...), kind=kOutput, calls=%fused_computation.9 | convolution fusion | flops 271253504 | bytes 17834496 | tf_op jit(solution)/shard_map/dot_general | solution.py:191
  173.7 3.3 %all-to-all-start.1 = ((f32[2,1,4096]{2,1,0:T(1,128)}), f32[2,1,4096]{2,1,0:T(1,128)S(1)}, u32[]{:S(2)}, u32[]{:S(2)}) async-start(f32[2,1,4096]{2,1,0:T(1,128)} %broadcast_in_dim.25), calls=%async_computation.1 | async-start | bytes 65536 | tf_op jit(solution)/shard_map/all_to_all | solution.py:29
  177.5 3.4 %all-to-all-done.1 = f32[2,1,4096]{2,1,0:T(1,128)S(1)} async-done(((f32[2,1,4096]{2,1,0:T(1,128)}), f32[2,1,4096]{2,1,0:T(1,128)S(1)}, u32[]{:S(2)}, u32[]{:S(2)}) %all-to-all-start.1) | async-done | bytes 32800 | tf_op jit(solution)/shard_map/all_to_all | solution.py:29
  (56 shorter events, 7.1 us)
Async XLA Ops:
  7.2 4.1 %copy-start = (bf16[256,1024]{1,0:T(8,128)(2,1)S(1)}, bf16[256,1024]{1,0:T(8,128)(2,1)}, u32[]{:S(2)}) copy-start(bf16[256,1024]{1,0:T(8,128)(2,1)} %param.21) | copy-start | bytes 1572868
  7.2 43.8 %all-gather.8.cloned.1.call-start = ((), (), s32[]{:S(2)}) async-start(), calls=%async_computation.3 | async-start | bytes 3145728 | tf_op jit(solution)/shard_map/all_gather | solution.py:112
  12.7 101.3 %all-gather.10.cloned.1.call-start = ((), (), s32[]{:S(2)}) async-start(), calls=%async_computation.4 | async-start | bytes 1310720 | tf_op jit(solution)/shard_map/all_gather | solution.py:46
  69.1 17.2 %copy-start.2 = (u32[128]{0:T(128)S(1)}, u32[128]{0:T(128)}, u32[]{:S(2)}) copy-start(u32[128]{0:T(128)} %constant.75) | copy-start | bytes 1540
  86.3 52.0 %all-gather.12.cloned.1.call-start = ((), (), s32[]{:S(2)}) async-start(), calls=%async_computation.5 | async-start | bytes 1310720 | tf_op jit(solution)/shard_map/all_gather | solution.py:46
  151.3 21.8 %all-to-all-start.2 = ((f32[2,1,3]{2,1,0:T(1,128)}), f32[2,1,3]{2,1,0:T(1,128)S(1)}, u32[]{:S(2)}, u32[]{:S(2)}) async-start(f32[2,1,3]{2,1,0:T(1,128)} %broadcast_in_dim.26), calls=%async_computation.2 | async-start | bytes 2048 | tf_op jit(solution)/shard_map/all_to_all | solution.py:29
  159.0 22.6 %copy-start.1 = (bf16[256,1024]{1,0:T(8,128)(2,1)S(1)}, bf16[256,1024]{1,0:T(8,128)(2,1)}, u32[]{:S(2)}) copy-start(bf16[256,1024]{1,0:T(8,128)(2,1)} %param.21) | copy-start | bytes 1572868
  173.7 7.2 %all-to-all-start.1 = ((f32[2,1,4096]{2,1,0:T(1,128)}), f32[2,1,4096]{2,1,0:T(1,128)S(1)}, u32[]{:S(2)}, u32[]{:S(2)}) async-start(f32[2,1,4096]{2,1,0:T(1,128)} %broadcast_in_dim.25), calls=%async_computation.1 | async-start | bytes 65536 | tf_op jit(solution)/shard_map/all_to_all | solution.py:29
Sparse Core Ops, SparseCore 0:
  12.9 38.0 all-gather.7
  86.4 25.2 all-gather.9
  116.1 22.1 all-gather.11
where the time goes:
time: 189 us; the launch traced here: 188 us
  blocking collectives  54.9 us (29%)
  matrix products  42.9 us (23%)
  waiting for transfers between devices  41.2 us (22%)
  other arithmetic  17.5 us (9%)
  between operations  14.6 us (8%)
  local copies, waits for them, and re-layouts  10.2 us (5%)
  starting transfers between devices  6.75 us (4%)
    all_gather x5, blocking collectives, combined_by_axis(): pieces = jax.tree.map(lambda part: lax.all_gather(part, axis), x)  27.9 us
    all_gather x1, waiting for transfers between devices, body(): lax.all_gather(x_samp, 'batch', axis=0, tiled=True)  26.6 us
    dot_general x1, matrix products, forward_critic(): preact = jnp.dot(rows_all, weight.T, preferred_element_type=jnp.float32)  18.1 us
    all_gather x2, waiting for transfers between devices, combined_by_axis(): pieces = jax.tree.map(lambda part: lax.all_gather(part, axis), x)  11.1 us
    unnamed x1, blocking collectives  10.7 us
    all_to_all x1, blocking collectives, copy_for_each(): lax.all_to_all(jnp.broadcast_to(x[None], (count, *x.shape)), axis, 0, 0,...  10.6 us
    reduce_sum x1, other arithmetic, body(): grad_v = grad_v + jnp.sum(dq_samp[:, None] * silu_out[data_hi:], axis=0)  9.14 us
    dot_general x1, matrix products, body(): jnp.dot(dpre_list.T, x_back, preferred_element_type=jnp.float32)  8.29 us
  transfers between devices with their start and end apart: 5, of which 3 were waited for; matrix products, arithmetic and copies ran while one was open for 19% of the time, Pallas kernels for 0%

commit v1 on v0

v1 whole, which is shorter than its diff:
```python
import jax
import jax.numpy as jnp
from jax import lax
from jax.experimental import pallas as pl
from jax.experimental.pallas import tpu as pltpu
from jax.sharding import Mesh
from jax.sharding import PartitionSpec as P

ENS = ("ens_0", "ens_1", "ens_2", "ens_3")
MESH_ID = pl.DeviceIdType.MESH
f32, bf16 = jnp.float32, jnp.bfloat16

D, H, HH = 1024, 4096, 2048
S, A, NACT = 32, 16, 256
ROWS = S * A
CH = 512
NCH = H // CH
TILE = 256
SUB = 32
PLANE = 32
COUNT = 64
discount, entropy_temp, penalty_weight, diversity_weight = 0.99, 0.2, 1.0, 1000.0

NN = (((1,), (0,)), ((), ()))
NT = (((1,), (1,)), ((), ()))
TN = (((0,), (0,)), ((), ()))


def dot(a, b, dims=NN):
    return lax.dot_general(a, b, dims, preferred_element_type=f32)


def mo(x, m):
    return pl.multiple_of(x, m)


def each(lo, hi, fn):
    def step(k, carry):
        fn(k)
        return carry

    lax.fori_loop(lo, hi, step, 0)


def iota(shape, dim):
    return lax.broadcasted_iota(jnp.int32, shape, dim)


def row8(x):
    return jnp.broadcast_to(x, (8, 128))


def main_kernel(
    obs_hbm, next_hbm, rows_hbm, dact_hbm, nact_hbm, sact_hbm, rew_hbm, logp_hbm, table_hbm, w_hbm, v_hbm,
    lhs_s, lhs_t, rhs_s, rhs_t, gw2_out, stats_out,
    tab_obs, tab_next, table, w, v, ids, sact, rl,
    xdn, xs, xd, tx_obs, rx_obs, tx_small, rx_small,
    vcol, gin, rx_g, tx_q, rx_q, units, rs_buf, q_buf, xr, xq, ag_tx, spread,
    h_buf, sl, silu, hd, q_sc, rx_qs, x_out, lt, rt, gw_part, gw2, stats_sc,
    in_sem, w_sem, out_sem, pair_s, pair_r, rs_s, rs_r, qs_s, qs_r, x_s, x_r, xq_s, xq_r, ag_s, ag_r,
):
    z, y, xh, core = (lax.axis_index(n) for n in ENS)
    b = lax.axis_index("batch")
    me = z * 8 + y * 2 + core
    xpos = xh * 2 + b

    def plane(k):
        j = lax.rem(me + k, PLANE)
        return j, (lax.div(j, 8), lax.rem(lax.div(j, 2), 4), xh, lax.rem(j, 2), b)

    def line(d):
        p = lax.rem(xpos + d, 4)
        return (z, y, lax.div(p, 2), core, lax.rem(p, 2))

    def tile_at(j):
        return pl.ds(mo(lax.div(j, 8) * 8, 8), 8), pl.ds(mo(lax.rem(j, 8) * 128, 128), 128)

    partner = (z, y, xh, core, 1 - b)
    h0 = mo(b * HH, HH)

    def far(src, dst, ssem, rsem, device):
        return pltpu.make_async_remote_copy(
            src_ref=src, dst_ref=dst, send_sem=ssem, recv_sem=rsem, device_id=device, device_id_type=MESH_ID
        )

    loads = [
        pltpu.make_async_copy(src, dst, in_sem.at[i])
        for i, (src, dst) in enumerate(
            [
                (rows_hbm, ids.at[0]), (dact_hbm, ids.at[1]), (nact_hbm, ids.at[2]), (sact_hbm, sact),
                (rew_hbm, rl.at[0]), (logp_hbm, rl.at[1]),
                (obs_hbm, tab_obs), (next_hbm, tab_next), (table_hbm, table), (v_hbm, v),
            ]
        )
    ]
    for c in loads:
        c.start()

    def w_copy(c):
        at = pl.ds(mo(c * CH, CH), CH)
        return pltpu.make_async_copy(w_hbm.at[at], w.at[at], w_sem.at[c])

    each(0, NCH, lambda c: w_copy(c).start())

    barrier = pltpu.get_barrier_semaphore()

    def greet(device):
        pl.semaphore_signal(barrier, inc=1, device_id=device, device_id_type=MESH_ID)

    each(1, PLANE, lambda k: greet(plane(k)[1]))
    for d in (1, 2, 3):
        greet(line(d))

    for c in loads:
        c.wait()

    lanes = iota((S, NACT), 1).astype(f32)
    eye = iota((S, S), 0) == iota((S, S), 1)
    ones = jnp.ones((S, NACT), bf16)

    def one_hot(i):
        diag = jnp.where(eye, jnp.broadcast_to(ids[i].astype(f32), (S, S)), 0.0).astype(bf16)
        return jnp.where(dot(diag, ones) == lanes, 1.0, 0.0).astype(bf16)

    def halved(x):
        return (x.astype(bf16).astype(f32) * 0.5).astype(bf16)

    own_oh = one_hot(0)
    obs = dot(own_oh, tab_obs[...])
    nxt = dot(own_oh, tab_next[...])
    tx_obs[...] = obs.astype(bf16)
    half_data = halved(obs + dot(one_hot(1), table[...]))
    xdn[0:S, :] = half_data
    xdn[S : 2 * S, :] = halved(nxt + dot(one_hot(2), table[...]))
    xd[0:S, :] = half_data
    tx_small[...] = jnp.zeros_like(tx_small)
    tx_small[0:A, 0:S] = sact[...].astype(f32)
    tx_small[A : A + 1, 0:S] = ids[1].astype(f32)
    tx_small[A + 1 : A + 2, 0:S] = rl[0]
    tx_small[A + 2 : A + 3, 0:S] = rl[1]

    def spread_v(i):
        at = pl.ds(mo(i * 128, 128), 128)
        vcol[at, :] = jnp.transpose(jnp.broadcast_to(v[:, at], (128, 128)))

    each(0, H // 128, spread_v)
    gin[...] = jnp.zeros_like(gin)

    def own_chunk(c, q_acc):
        w_copy(c).wait()
        at = pl.ds(mo(c * CH, CH), CH)
        wc = w[at, :]
        h = dot(wc, xdn[...], NT)
        th = jnp.tanh(h)
        a = h * th
        vc = vcol[at, 0 : 2 * S]
        q_acc = q_acc + jnp.sum((h + a) * vc, axis=0, keepdims=True)
        co = (0.5 * vc * ((1.0 + th) + (h - a * th))).astype(bf16)
        gin[...] += dot(co[:, 0:S], wc, TN)
        return q_acc

    q_own = lax.fori_loop(0, NCH // 2, own_chunk, jnp.zeros((1, 2 * S), f32))
    pl.semaphore_wait(barrier, PLANE - 1 + 3)
    cp_obs = far(tx_obs, rx_obs, pair_s.at[0], pair_r.at[0], partner)
    cp_small = far(tx_small, rx_small, pair_s.at[1], pair_r.at[1], partner)
    cp_obs.start()
    cp_small.start()
    q_own = lax.fori_loop(NCH // 2, NCH, own_chunk, q_own)

    tx_q[...] = jnp.zeros_like(tx_q)
    tx_q[:, 0 : 2 * S] = q_own

    def norm_of(g):
        return jnp.sqrt(jnp.sum(g * g, axis=-1, keepdims=True) + 1.0)

    g_own = gin[...]
    norm_own = norm_of(g_own)
    units[0:S, :] = g_own / norm_own

    def rs_copy(k):
        j, device = plane(k)
        r, c = tile_at(j)
        return far(units.at[r, c], rs_buf.at[k], rs_s.at[k], rs_r.at[k], device)

    def qs_copy(k):
        return far(tx_q, q_buf.at[k], qs_s.at[k], qs_r.at[k], plane(k)[1])

    each(1, PLANE, lambda k: rs_copy(k).start())
    each(1, PLANE, lambda k: qs_copy(k).start())
    cp_g = far(gin, rx_g, pair_s.at[2], pair_r.at[2], partner)
    cp_q = far(tx_q, rx_q, pair_s.at[3], pair_r.at[3], partner)
    cp_g.start()
    cp_q.start()

    def build(sact_f, base, off):
        row = iota((ROWS, S), 0)
        pick = jnp.where((row & (S - 1)) == iota((ROWS, S), 1), 1.0, 0.0).astype(bf16)
        each_sample = dot(pick, sact_f.astype(bf16), NT)
        mine = lax.shift_right_logical(iota((ROWS, A), 0), 5) == iota((ROWS, A), 1)
        index = dot(jnp.where(mine, each_sample, 0.0).astype(bf16), jnp.ones((A, NACT), bf16))
        oh = jnp.where(index == iota((ROWS, NACT), 1).astype(f32), 1.0, 0.0).astype(bf16)
        for i in range(A):
            part = dot(oh[i * S : (i + 1) * S], table[...])
            xs[off + i * S : off + (i + 1) * S, :] = halved(base + part)

    def forward(n):
        at = pl.ds(mo(n * TILE, TILE), TILE)
        h_buf[...] = dot(w[pl.ds(h0, HH), :], xs[at, :], NT)

        def sub(i, q):
            r = pl.ds(mo(i * SUB, SUB), SUB)
            h = h_buf[r, :]
            th = jnp.tanh(h)
            a = h * th
            vc = vcol[pl.ds(mo(h0 + i * SUB, SUB), SUB), :]
            v2 = jnp.concatenate([vc, vc], axis=1)
            so = h + a
            silu[r, at] = so.astype(bf16)
            sl[r, at] = (0.5 * v2 * ((1.0 + th) + (h - a * th))).astype(bf16)
            sv = so * v2
            return q + ((sv[0:8] + sv[8:16]) + (sv[16:24] + sv[24:32]))

        q = lax.fori_loop(0, HH // SUB, sub, jnp.zeros((8, TILE), f32), unroll=4)
        q = jnp.sum(q, axis=0, keepdims=True)
        q_sc[pl.ds(2 * n, 1), :] = q[:, 0:128]
        q_sc[pl.ds(2 * n + 1, 1), :] = q[:, 128:256]

    build(sact[...].astype(f32), obs, 0)
    each(0, 2, forward)

    each(1, PLANE, lambda k: rs_copy(k).wait_recv())
    each(1, PLANE, lambda k: qs_copy(k).wait_recv())
    r_me, c_me = tile_at(me)
    rs_buf[0] = units[r_me, c_me]
    q_buf[0] = tx_q[...]
    xr[0] = jnp.sum(rs_buf[...], axis=0)
    xq[0] = jnp.min(q_buf[...], axis=0)
    x_copies = []
    for d in (1, 2, 3):
        x_copies.append(far(xr.at[0], xr.at[d], x_s.at[d], x_r.at[d], line(d)))
        x_copies.append(far(xq.at[0], xq.at[d], xq_s.at[d], xq_r.at[d], line(d)))
    for c in x_copies:
        c.start()

    cp_obs.wait_recv()
    cp_small.wait_recv()
    obs_p = rx_obs[...].astype(f32)
    build(rx_small[0:A, 0:S], obs_p, ROWS)
    diag = jnp.where(eye, jnp.broadcast_to(rx_small[A : A + 1, 0:S], (S, S)), 0.0).astype(bf16)
    oh_p = jnp.where(dot(diag, ones) == lanes, 1.0, 0.0).astype(bf16)
    xd[S : 2 * S, :] = halved(obs_p + dot(oh_p, table[...]))
    each(2, 3, forward)

    for c in x_copies:
        c.wait_recv()
    ag_tx[0] = xr[0] + xr[2]
    ag_tx[1] = xr[1] + xr[3]

    def ag_copy(k):
        return far(ag_tx, spread.at[:, r_me, c_me], ag_s.at[k], ag_r.at[k], plane(k)[1])

    each(1, PLANE, lambda k: ag_copy(k).start())
    spread[:, r_me, c_me] = ag_tx[...]

    each(3, 4, forward)
    hd[...] = dot(w[pl.ds(h0, HH), :], xd[...], NT)
    cp_qs = far(q_sc, rx_qs, pair_s.at[4], pair_r.at[4], partner)
    cp_qs.start()
    out_l = pltpu.make_async_copy(sl, lhs_s, out_sem.at[0])
    out_l.start()

    cp_g.wait_recv()
    g_p = rx_g[...]
    norm_p = norm_of(g_p)
    units[S : 2 * S, :] = g_p / norm_p
    rt[0:COUNT, :] = (xd[...].astype(f32) * 2.0).astype(bf16)

    cp_qs.wait_recv()
    q_all = jnp.concatenate([q_sc[0:4] + rx_qs[4:8], q_sc[4:8] + rx_qs[0:4]], axis=0)
    e = jnp.exp(q_all)

    def mass(rows):
        m = row8(jnp.sum(rows, axis=0, keepdims=True))
        m = m + pltpu.roll(m, 32, 1)
        return jnp.log(m + pltpu.roll(m, 64, 1))

    mass_own, mass_p = mass(e[0:4]), mass(e[4:8])
    sub_row = iota((8, 128), 0)
    lane = iota((8, 128), 1)
    dq = jnp.exp(q_all - jnp.where(sub_row < 4, mass_own, mass_p)) * (penalty_weight / COUNT)
    for r in range(8):
        col = jnp.transpose(jnp.broadcast_to(dq[r : r + 1, :], (128, 128))) * 2.0
        for c in range(8):
            part = xs[r * 128 : (r + 1) * 128, c * 128 : (c + 1) * 128].astype(f32) * col
            x_out[r * 128 : (r + 1) * 128, c * 128 : (c + 1) * 128] = part.astype(bf16)
    out_r = pltpu.make_async_copy(x_out, rhs_s, out_sem.at[1])
    out_r.start()

    def penalty_part(i):
        r = pl.ds(mo(i * SUB, SUB), SUB)
        acc = jnp.zeros((SUB, 128), f32)
        for k in range(8):
            acc = acc + silu[r, k * 128 : (k + 1) * 128].astype(f32) * dq[k : k + 1, :]
        gw_part[r, :] = acc

    each(0, HH // SUB, penalty_part)

    cp_q.wait_recv()
    left = lane < S

    def both(own, other):
        return jnp.where(left, own, other)

    floor = both(pltpu.roll(row8(jnp.minimum(xq[0], xq[2])), 96, 1), row8(jnp.minimum(xq[1], xq[3])))
    q_data = both(row8(tx_q[...]), pltpu.roll(row8(rx_q[...]), 32, 1))
    rew = both(row8(tx_small[A + 1 : A + 2, :]), pltpu.roll(row8(rx_small[A + 1 : A + 2, :]), 32, 1))
    logp = both(row8(tx_small[A + 2 : A + 3, :]), pltpu.roll(row8(rx_small[A + 2 : A + 3, :]), 32, 1))
    target = rew + discount * (floor - entropy_temp * logp)
    td_gap = q_data - target
    dq_data = ((2.0 * td_gap - penalty_weight) * (1.0 / COUNT))[0:1, 0:COUNT]
    gap_terms = td_gap * td_gap
    mass_terms = both(mass_own, mass_p) - q_data

    each(1, PLANE, lambda k: ag_copy(k).wait_recv())
    unit = units[...]
    rest = spread[...].reshape(COUNT, D) - unit
    div_row = jnp.sum(unit * rest, axis=-1, keepdims=True)
    scale = 2.0 * diversity_weight / (COUNT - 1) / COUNT
    norms = jnp.concatenate([norm_own, norm_p], axis=0)
    dgrad = ((scale * rest - unit * (scale * div_row)) / norms).astype(bf16)
    rt[COUNT : 2 * COUNT, :] = dgrad

    def total(row):
        return jnp.sum(jnp.where(lane < COUNT, row, 0.0)[0:1], axis=1, keepdims=True)

    div_sum = jnp.sum(div_row, axis=0, keepdims=True)
    stats = jnp.where(
        lane[0:1] == 0, total(gap_terms), jnp.where(lane[0:1] == 1, total(mass_terms), div_sum)
    )
    stats_sc[...] = stats * (1.0 / COUNT)

    def tail(i):
        r = pl.ds(mo(i * 256, 256), 256)
        dc = dot(w[pl.ds(mo(h0 + i * 256, 256), 256), :], dgrad, NT)
        h = hd[r, :]
        th = jnp.tanh(h)
        a = h * th
        vc = vcol[pl.ds(mo(h0 + i * 256, 256), 256), 0:COUNT]
        slope = 0.5 * ((1.0 + th) + (h - a * th))
        curve = 0.5 * (1.0 - th * th) * (1.0 - a)
        dpre = (vc * (dq_data * slope + dc * curve)).astype(bf16)
        lt[r, :] = jnp.concatenate([dpre, (vc * slope).astype(bf16)], axis=1)
        gw_part[r, 0:COUNT] += dq_data * (h + a) + dc * slope
        for k in range(2):
            rows = pl.ds(mo(i * 256 + k * 128, 128), 128)
            gw2[b, pl.ds(2 * i + k, 1), :] = jnp.sum(jnp.transpose(gw_part[rows, :]), axis=0, keepdims=True)

    each(0, HH // 256, tail)
    cp_gw = far(gw2.at[b], gw2.at[b], pair_s.at[5], pair_r.at[5], partner)
    cp_gw.start()
    outs = [
        pltpu.make_async_copy(lt, lhs_t, out_sem.at[2]),
        pltpu.make_async_copy(rt, rhs_t, out_sem.at[3]),
        pltpu.make_async_copy(stats_sc, stats_out, out_sem.at[4]),
    ]
    for c in outs:
        c.start()
    each(1, PLANE, lambda k: rs_copy(k).wait_send())
    each(1, PLANE, lambda k: qs_copy(k).wait_send())
    each(1, PLANE, lambda k: ag_copy(k).wait_send())
    for c in x_copies + [cp_obs, cp_small, cp_g, cp_q, cp_qs]:
        c.wait_send()
    cp_gw.wait()
    out_g = pltpu.make_async_copy(gw2, gw2_out, out_sem.at[5])
    out_g.start()
    for c in outs + [out_l, out_r, out_g]:
        c.wait()


def run_main(*args):
    sds = jax.ShapeDtypeStruct
    outs = [
        sds((HH, 2 * ROWS), bf16), sds((HH, 2 * COUNT), bf16), sds((2 * ROWS, D), bf16), sds((2 * COUNT, D), bf16),
        sds((2, HH // 128, 128), f32), sds((1, 128), f32),
    ]
    vm, dma = pltpu.VMEM, pltpu.SemaphoreType.DMA
    scratch = [
        vm((NACT, D), bf16), vm((NACT, D), bf16), vm((NACT, D), bf16), vm((H, D), bf16), vm((1, H), f32),
        vm((3, 1, S), jnp.int32), vm((A, S), jnp.int32), vm((2, 1, S), f32),
        vm((2 * S, D), bf16), vm((2 * ROWS, D), bf16), vm((2 * S, D), bf16),
        vm((S, D), bf16), vm((S, D), bf16), vm((24, 128), f32), vm((24, 128), f32),
        vm((H, 128), f32), vm((S, D), f32), vm((S, D), f32), vm((1, 128), f32), vm((1, 128), f32),
        vm((COUNT, D), f32), vm((PLANE, 8, 128), f32), vm((PLANE, 1, 128), f32),
        vm((4, 8, 128), f32), vm((4, 1, 128), f32), vm((2, 8, 128), f32), vm((2, S, D), f32),
        vm((HH, TILE), f32), vm((HH, 2 * ROWS), bf16), vm((HH, 2 * ROWS), bf16), vm((HH, COUNT), f32),
        vm((8, 128), f32), vm((8, 128), f32), vm((2 * ROWS, D), bf16),
        vm((HH, 2 * COUNT), bf16), vm((2 * COUNT, D), bf16), vm((HH, 128), f32),
        vm((2, HH // 128, 128), f32), vm((1, 128), f32),
        dma((10,)), dma((NCH,)), dma((6,)), dma((6,)), dma((6,)),
        dma((PLANE,)), dma((PLANE,)), dma((PLANE,)), dma((PLANE,)),
        dma((4,)), dma((4,)), dma((4,)), dma((4,)), dma((PLANE,)), dma((PLANE,)),
    ]
    any_spec = pl.BlockSpec(memory_space=pl.ANY)
    return pl.pallas_call(
        main_kernel,
        out_shape=outs,
        in_specs=[any_spec] * len(args),
        out_specs=[any_spec] * len(outs),
        scratch_shapes=scratch,
        compiler_params=pltpu.CompilerParams(collective_id=0, has_side_effects=True, vmem_limit_bytes=60 << 20),
        name="critics",
    )(*args)


STEP = 512


def weight_kernel(lhs_s, lhs_t, rhs_s, rhs_t, gw2_in, stats_in, out, gw2, stats):
    out[0] = dot(lhs_s[...], rhs_s[...]) + dot(lhs_t[...], rhs_t[...])

    @pl.when(pl.program_id(0) == 0)
    def _():
        for k in range(2):
            for i in range(HH // 128):
                at = k * HH + i * 128
                gw2[:, at : at + 128] = gw2_in[k, i : i + 1, :]
        stats[...] = stats_in[:, 0:3]


def run_weight(*args):
    sds = jax.ShapeDtypeStruct
    once = pl.Buffered(1)
    whole = lambda *shape: pl.BlockSpec(shape, lambda i: (0,) * len(shape), pipeline_mode=once)
    return pl.pallas_call(
        weight_kernel,
        grid=(HH // STEP,),
        out_shape=[sds((1, HH, D), f32), sds((1, H), f32), sds((1, 3), f32)],
        in_specs=[
            pl.BlockSpec((STEP, 2 * ROWS), lambda i: (i, 0)),
            pl.BlockSpec((STEP, 2 * COUNT), lambda i: (i, 0)),
            whole(2 * ROWS, D), whole(2 * COUNT, D), whole(2, HH // 128, 128), whole(1, 128),
        ],
        out_specs=[
            pl.BlockSpec((1, STEP, D), lambda i: (0, i, 0)),
            pl.BlockSpec((1, H), lambda i: (0, 0)),
            pl.BlockSpec((1, 3), lambda i: (0, 0)),
        ],
        name="weights",
    )(*args)


def body(
    replay_obs, replay_next, batch_rows, data_action, next_action, sampled_actions,
    reward, next_logp, action_table, w1, w2,
):
    row = lambda x: x.reshape(1, S)
    parts = run_main(
        replay_obs, replay_next, row(batch_rows), row(data_action), row(next_action), sampled_actions.T,
        row(reward), row(next_logp), action_table, w1.reshape(H, D), w2,
    )
    return run_weight(*parts)


def solution(mesh):
    finer = Mesh(mesh.devices.reshape(4, 4, 2, 2, mesh.shape["batch"]), (*ENS, "batch"))
    placed = (
        P("batch", None), P("batch", None), P("batch"), P("batch"), P("batch"), P("batch", None),
        P("batch"), P("batch"), P(), P(ENS, None, None), P(ENS, None),
    )
    return jax.shard_map(
        body,
        mesh=finer,
        in_specs=placed,
        out_specs=(P(ENS, "batch", None), P(ENS, None), P(ENS, None)),
        check_vma=False,
    )
```

time: 189 us -> 57.2 us (0.30)
  Pallas kernels: 0 us -> 56.3 us
  blocking collectives: 54.9 us -> 0 us
  matrix products: 42.9 us -> 0 us
  waiting for transfers between devices: 41.2 us -> 0 us
  other arithmetic: 17.5 us -> 0 us
  between operations: 14.6 us -> 0.64 us
  local copies, waits for them, and re-layouts: 10.2 us -> 0 us
  starting transfers between devices: 6.75 us -> 0 us
    pallas_call x0 -> x2, Pallas kernels: none -> 56.3 us  [the longest x1 46.3 us: run_main(): pl.pallas_call(main_kernel, out_shape=outs, in_specs=[any_spec] * len(arg...]
    dot_general x8 -> x0, matrix products: 42.9 us -> none  [the longest x1 18.1 us: forward_critic(): preact = jnp.dot(rows_all, weight.T, preferred_element_type=jnp.float32)]
    all_gather x3 -> x0, waiting for transfers between devices: 37.7 us -> none  [the longest x1 26.6 us: body(): lax.all_gather(x_samp, 'batch', axis=0, tiled=True)]
    all_gather x6 -> x0, blocking collectives: 33.7 us -> none  [the longest x5 27.9 us: combined_by_axis(): pieces = jax.tree.map(lambda part: lax.all_gather(part, axis), x)]
    reduce_sum x8 -> x0, other arithmetic: 11.2 us -> none  [the longest x1 9.14 us: body(): grad_v = grad_v + jnp.sum(dq_samp[:, None] * silu_out[data_hi:], axis=0)]
    unnamed x1 -> x0, blocking collectives: 10.7 us -> none
    all_to_all x1 -> x0, blocking collectives: 10.6 us -> none  [copy_for_each(): lax.all_to_all(jnp.broadcast_to(x[None], (count, *x.shape)), axis, 0, 0,...]
    all_to_all x2 -> x0, starting transfers between devices: 6.63 us -> none  [copy_for_each(): lax.all_to_all(jnp.broadcast_to(x[None], (count, *x.shape)), axis, 0, 0,...]
  transfers between devices with their start and end apart: 5 -> 0, of which waited for: 3 -> 0; matrix products, arithmetic and copies ran while one was open for 19% -> 0% of each run, Pallas kernels for 0% -> 0%
where the time goes in v1:
time: 57.2 us; the launch traced here: 57 us
  Pallas kernels  56.3 us (98%)
  between operations  0.64 us (1%)
    pallas_call x1, Pallas kernels, run_main(): pl.pallas_call(main_kernel, out_shape=outs, in_specs=[any_spec] * len(arg...  46.3 us
    pallas_call x1, Pallas kernels, run_weight(): pl.pallas_call(weight_kernel, grid=(HH // STEP,), out_shape=[sds((1, HH,...  10 us

profile of v1, /device:TPU:0, one launch (start us, length us, event | category | flops | bytes accessed | tf_op | source)
XLA Modules:
  0.0 57.0 jit_solution(15472967505955309333)
XLA Ops:
  0.6 46.3 %critics.1 = (bf16[2048,1024]{1,0:T(8,128)(2,1)}, bf16[2048,128]{1,0:T(8,128)(2,1)}, bf16[1024,1024]{1,0:T(8,128)(2,1)}, bf16[128,1024]{1,0:T(8,128)(2,1)}, f32[2,16,128]{2,1,0:T(8,128)}, /*index=5*/f32[1,128]{1,0:T(1,128)}) custom-call(bf16[256,1024]{1,0:T(8,128)(2,1)} %obs_hbm.1, bf16[256,1024]{1,0:T(8,128)(2,1)} %next_hbm.1, s32[1,32]{1,0:T(1,128)} %bitcast.9, ...), custom_call_target="tpu_custom_call" | custom-call | tf_op jit(solution)/shard_map/critics/pallas_call | solution.py:404
  46.9 10.0 %weights.1 = (f32[1,2048,1024]{2,1,0:T(8,128)}, f32[1,4096]{1,0:T(1,128)}, f32[1,3]{1,0:T(1,128)}) custom-call(bf16[2048,1024]{1,0:T(8,128)(2,1)} %get-tuple-element.9.lhs_s, bf16[2048,128]{1,0:T(8,128)(2,1)} %get-tuple-element.10.lhs_t, bf16[1024,1024]{1,0:T(8,128)(2,1)} %get-tuple-element.11.rhs_s, bf16[128,1024]{1,0:T(8,128)(2,1)} %get-tuple-element.12.rhs_t, ...), custom_call_target="tpu_custom_call" | custom-call | tf_op jit(solution)/shard_map/weights/pallas_call | solution.py:434

commit v2 on v1

v2 whole, which is shorter than its diff:
```python
import jax
import jax.numpy as jnp
from jax import lax
from jax.experimental import pallas as pl
from jax.experimental.pallas import tpu as pltpu
from jax.sharding import Mesh
from jax.sharding import PartitionSpec as P

ENS = ("ens_0", "ens_1", "ens_2", "ens_3")
MESH_ID = pl.DeviceIdType.MESH
f32, bf16 = jnp.float32, jnp.bfloat16

D, H, HH = 1024, 4096, 2048
S, A, NACT = 32, 16, 256
ROWS = S * A
CH = 1024
NCH = H // CH
BLK = 512
SUB = 32
PLANE = 32
COUNT = 64
discount, entropy_temp, penalty_weight, diversity_weight = 0.99, 0.2, 1.0, 1000.0

NN = (((1,), (0,)), ((), ()))
NT = (((1,), (1,)), ((), ()))
TN = (((0,), (0,)), ((), ()))


def dot(a, b, dims=NN):
    return lax.dot_general(a, b, dims, preferred_element_type=f32)


def mo(x, m):
    return pl.multiple_of(x, m)


def each(lo, hi, fn):
    def step(k, carry):
        fn(k)
        return carry

    lax.fori_loop(lo, hi, step, 0)


def iota(shape, dim):
    return lax.broadcasted_iota(jnp.int32, shape, dim)


def row8(x):
    return jnp.broadcast_to(x, (8, 128))


def main_kernel(
    obs_hbm, next_hbm, rows_hbm, dact_hbm, nact_hbm, sact_hbm, rew_hbm, logp_hbm, table_hbm, w_hbm, v_hbm,
    part, lt, rt, gw2, stats_out,
    tab_obs, tab_next, table, w, v, ids, sact, rl,
    xdn, xs, xd, tx_obs, rx_obs, tx_small, rx_small,
    vcol, ho, gin, rx_g, tx_q, rx_q, units, rs_tx, rs_buf, xr, ag_tx, spread,
    h_buf, sl, silu, q_sc, rx_qs, x_out, tail_x, tail_r,
    in_sem, w_sem, pair_s, pair_r, rs_s, rs_r, x_s, x_r, ag_s, ag_r,
):
    z, y, xh, core = (lax.axis_index(n) for n in ENS)
    b = lax.axis_index("batch")
    me = z * 8 + y * 2 + core
    xpos = xh * 2 + b

    def plane(k):
        j = lax.rem(me + k, PLANE)
        return j, (lax.div(j, 8), lax.rem(lax.div(j, 2), 4), xh, lax.rem(j, 2), b)

    def line(d):
        p = lax.rem(xpos + d, 4)
        return (z, y, lax.div(p, 2), core, lax.rem(p, 2))

    partner = (z, y, xh, core, 1 - b)
    h0 = mo(b * HH, HH)

    def far(src, dst, ssem, rsem, device):
        return pltpu.make_async_remote_copy(
            src_ref=src, dst_ref=dst, send_sem=ssem, recv_sem=rsem, device_id=device, device_id_type=MESH_ID
        )

    loads = [
        pltpu.make_async_copy(src, dst, in_sem.at[i])
        for i, (src, dst) in enumerate(
            [
                (rows_hbm, ids.at[0]), (dact_hbm, ids.at[1]), (nact_hbm, ids.at[2]), (sact_hbm, sact),
                (rew_hbm, rl.at[0]), (logp_hbm, rl.at[1]),
                (obs_hbm, tab_obs), (table_hbm, table), (next_hbm, tab_next), (v_hbm, v),
            ]
        )
    ]
    for c in loads:
        c.start()

    def w_copy(c):
        at = pl.ds(c * CH, CH)
        return pltpu.make_async_copy(w_hbm.at[at], w.at[at], w_sem.at[c])

    for c in range(NCH):
        w_copy(c).start()

    barrier = pltpu.get_barrier_semaphore()

    def greet(device):
        pl.semaphore_signal(barrier, inc=1, device_id=device, device_id_type=MESH_ID)

    each(1, PLANE, lambda k: greet(plane(k)[1]))
    for d in (1, 2, 3):
        greet(line(d))

    for c in loads[:6]:
        c.wait()

    lanes = iota((S, NACT), 1).astype(f32)
    eye = iota((S, S), 0) == iota((S, S), 1)
    ones = jnp.ones((S, NACT), bf16)

    def one_hot(row, value):
        diag = jnp.where(eye, jnp.broadcast_to(row, (S, S)), 0.0).astype(bf16)
        return jnp.where(dot(diag, ones) == lanes, value, 0.0).astype(bf16)

    def sample_hot(sact_f):
        pick = jnp.where((iota((ROWS, S), 0) & (S - 1)) == iota((ROWS, S), 1), 1.0, 0.0).astype(bf16)
        each_sample = dot(pick, sact_f.astype(bf16), NT)
        mine = lax.shift_right_logical(iota((ROWS, A), 0), 5) == iota((ROWS, A), 1)
        index = dot(jnp.where(mine, each_sample, 0.0).astype(bf16), jnp.ones((A, NACT), bf16))
        return jnp.where(index == iota((ROWS, NACT), 1).astype(f32), 0.5, 0.0).astype(bf16)

    rows_oh, dact_oh, nact_oh = (one_hot(ids[i].astype(f32), 0.5) for i in range(3))
    own_hot = sample_hot(sact[...].astype(f32))
    tx_small[...] = jnp.zeros_like(tx_small)
    tx_small[0:A, 0:S] = sact[...].astype(f32)
    tx_small[A : A + 1, 0:S] = ids[1].astype(f32)
    tx_small[A + 1 : A + 2, 0:S] = rl[0]
    tx_small[A + 2 : A + 3, 0:S] = rl[1]
    for c in loads[6:]:
        c.wait()

    obs = dot(rows_oh, tab_obs[...])
    nxt = dot(rows_oh, tab_next[...])
    tx_obs[...] = obs.astype(bf16)
    half_data = (obs + dot(dact_oh, table[...])).astype(bf16)
    xdn[0:S, :] = half_data
    xdn[S : 2 * S, :] = (nxt + dot(nact_oh, table[...])).astype(bf16)
    xd[0:S, :] = half_data

    def own_act(c, q_acc):
        at = slice(c * CH, (c + 1) * CH)
        h = ho[:, at]
        th = jnp.tanh(h)
        a = h * th
        vr = v[:, at]
        sv = (h + a) * vr
        for k in range(CH // 128):
            q_acc = q_acc + sv[:, k * 128 : (k + 1) * 128]
        hs, ts = h[0:S], th[0:S]
        co = (0.5 * vr * ((1.0 + ts) + (hs - a[0:S] * ts))).astype(bf16)
        g = dot(co, w[at, :])
        gin[...] = g if c == 0 else gin[...] + g
        return q_acc

    def spread_v(i):
        at = pl.ds(mo(h0 + i * 128, 128), 128)
        vcol[i * 128 : (i + 1) * 128, :] = jnp.transpose(jnp.broadcast_to(v[:, at], (128, 128)))

    q_acc = jnp.zeros((2 * S, 128), f32)
    cp_obs = far(tx_obs, rx_obs, pair_s.at[0], pair_r.at[0], partner)
    cp_small = far(tx_small, rx_small, pair_s.at[1], pair_r.at[1], partner)
    for c in range(NCH):
        w_copy(c).wait()
        ho[:, c * CH : (c + 1) * CH] = dot(xdn[...], w[c * CH : (c + 1) * CH, :], NT)
        if c > 0:
            q_acc = own_act(c - 1, q_acc)
        for i in range(4):
            spread_v(4 * c + i)
        if c == 2:
            pl.semaphore_wait(barrier, PLANE - 1 + 3)
            cp_obs.start()
            cp_small.start()
    q_acc = own_act(NCH - 1, q_acc)
    q_own = jnp.sum(jnp.transpose(jnp.concatenate([q_acc, jnp.zeros((64, 128), f32)], axis=0)), axis=0, keepdims=True)
    tx_q[...] = q_own

    def norm_of(g):
        return jnp.sqrt(jnp.sum(g * g, axis=-1, keepdims=True) + 1.0)

    g_own = gin[...]
    norm_own = norm_of(g_own)
    u_own = g_own / norm_own
    units[0:S, :] = u_own
    for j in range(PLANE):
        r, c = j // 8, j % 8
        rs_tx[j, 0:8, :] = u_own[8 * r : 8 * r + 8, 128 * c : 128 * c + 128]
        rs_tx[j, 8:9, :] = q_own

    def rs_copy(k):
        j, device = plane(k)
        return far(rs_tx.at[j], rs_buf.at[k], rs_s.at[k], rs_r.at[k], device)

    each(1, PLANE, lambda k: rs_copy(k).start())
    cp_g = far(gin, rx_g, pair_s.at[2], pair_r.at[2], partner)
    cp_q = far(tx_q, rx_q, pair_s.at[3], pair_r.at[3], partner)
    cp_g.start()
    cp_q.start()

    def build(hot, base, off):
        for p in range(2):
            h_buf[p] = dot(hot, table[:, p * 512 : (p + 1) * 512])
        for i in range(A):
            for p in range(2):
                x = (base[:, p * 512 : (p + 1) * 512] + h_buf[p, i * S : (i + 1) * S, :]).astype(bf16)
                xs[off + i * S : off + (i + 1) * S, p * 512 : (p + 1) * 512] = x

    def product(m, half):
        h_buf[m % 2] = dot(w[pl.ds(mo(h0 + m * BLK, BLK), BLK), :], xs[half * ROWS : (half + 1) * ROWS, :], NT)

    def activate(m, half, q):
        at = slice(half * ROWS, (half + 1) * ROWS)
        for i in range(BLK // SUB):
            h = h_buf[m % 2, i * SUB : (i + 1) * SUB, :]
            r = slice(m * BLK + i * SUB, m * BLK + (i + 1) * SUB)
            th = jnp.tanh(h)
            a = h * th
            vc = vcol[r, :]
            v4 = jnp.concatenate([vc, vc, vc, vc], axis=1)
            so = h + a
            silu[r, at] = so.astype(bf16)
            sl[r, at] = (0.5 * v4 * ((1.0 + th) + (h - a * th))).astype(bf16)
            sv = so * v4
            q = q + ((sv[0:8] + sv[8:16]) + (sv[16:24] + sv[24:32]))
        return q

    def keep_q(q, half):
        q = jnp.sum(q, axis=0, keepdims=True)
        for k in range(4):
            q_sc[4 * half + k : 4 * half + k + 1, :] = q[:, k * 128 : (k + 1) * 128]

    nb = HH // BLK
    q_zero = jnp.zeros((8, ROWS), f32)

    def forward(half):
        product(0, half)
        q = q_zero
        for m in range(1, nb):
            product(m, half)
            q = activate(m - 1, half, q)
        keep_q(activate(nb - 1, half, q), half)

    build(own_hot, obs, 0)
    forward(0)

    cp_obs.wait_recv()
    cp_small.wait_recv()
    obs_p = rx_obs[...].astype(f32)
    build(sample_hot(rx_small[0:A, 0:S]), obs_p, ROWS)
    half_p = (obs_p + dot(one_hot(rx_small[A : A + 1, 0:S], 0.5), table[...])).astype(bf16)
    xd[S : 2 * S, :] = half_p
    tail_x[COUNT : COUNT + S, :] = half_p
    forward(1)
    cp_qs = far(q_sc, rx_qs, pair_s.at[4], pair_r.at[4], partner)
    cp_qs.start()

    each(1, PLANE, lambda k: rs_copy(k).wait_recv())
    rs_buf[0] = rs_tx[me]
    got = rs_buf[...]
    xr[0, 0:8, :] = jnp.sum(got[:, 0:8, :], axis=0)
    xr[0, 8:9, :] = jnp.min(got[:, 8:9, :], axis=0)
    x_copies = [far(xr.at[0], xr.at[d], x_s.at[d], x_r.at[d], line(d)) for d in (1, 2, 3)]
    for c in x_copies:
        c.start()

    cp_g.wait_recv()
    g_p = rx_g[...]
    norm_p = norm_of(g_p)
    units[S : 2 * S, :] = g_p / norm_p
    rt[0:COUNT, :] = (xd[...].astype(f32) * 2.0).astype(bf16)

    cp_qs.wait_recv()
    q_all = jnp.concatenate([q_sc[0:4] + rx_qs[4:8], q_sc[4:8] + rx_qs[0:4]], axis=0)
    e = jnp.exp(q_all)

    def mass(rows):
        m = row8(jnp.sum(rows, axis=0, keepdims=True))
        m = m + pltpu.roll(m, 32, 1)
        return jnp.log(m + pltpu.roll(m, 64, 1))

    mass_own, mass_p = mass(e[0:4]), mass(e[4:8])
    sub_row = iota((8, 128), 0)
    lane = iota((8, 128), 1)
    dq = jnp.exp(q_all - jnp.where(sub_row < 4, mass_own, mass_p)) * (penalty_weight / COUNT)
    for r in range(8):
        col = jnp.transpose(jnp.broadcast_to(dq[r : r + 1, :], (128, 128))) * 2.0
        for c in range(8):
            scaled = xs[r * 128 : (r + 1) * 128, c * 128 : (c + 1) * 128].astype(f32) * col
            x_out[r * 128 : (r + 1) * 128, c * 128 : (c + 1) * 128] = scaled.astype(bf16)

    for c in x_copies:
        c.wait_recv()
    row_me = mo(lax.div(me, 8) * 16, 16)
    col_me = mo(lax.rem(me, 8) * 128, 128)
    ag_tx[...] = jnp.concatenate([xr[0, 0:8, :] + xr[2, 0:8, :], xr[1, 0:8, :] + xr[3, 0:8, :]], axis=0).astype(bf16)

    def ag_copy(k):
        dst = spread.at[pl.ds(row_me, 16), pl.ds(col_me, 128)]
        return far(ag_tx, dst, ag_s.at[k], ag_r.at[k], plane(k)[1])

    each(1, PLANE, lambda k: ag_copy(k).start())
    spread[pl.ds(row_me, 16), pl.ds(col_me, 128)] = ag_tx[...]

    dq_row = jnp.concatenate([dq[r : r + 1, :] for r in range(8)], axis=1)
    dq_hi = dq_row.astype(bf16).astype(f32)
    dq_two = jnp.concatenate([dq_hi, dq_row - dq_hi, jnp.zeros((14, 2 * ROWS), f32)], axis=0).astype(bf16)
    gw_s = dot(dq_two, silu[...], NT)
    gw_s = gw_s[0:1] + gw_s[1:2]
    for m in range(nb):
        r = slice(m * BLK, (m + 1) * BLK)
        part[r, :] = dot(sl[r, :], x_out[...])

    cp_q.wait_recv()
    left = lane < S

    def both(own, other):
        return jnp.where(left, own, other)

    floor_own, floor_p = jnp.minimum(xr[0, 8:9, :], xr[2, 8:9, :]), jnp.minimum(xr[1, 8:9, :], xr[3, 8:9, :])
    floor = both(pltpu.roll(row8(floor_own), 96, 1), row8(floor_p))
    q_data = both(row8(tx_q[...]), pltpu.roll(row8(rx_q[...]), 32, 1))
    rew = both(row8(tx_small[A + 1 : A + 2, :]), pltpu.roll(row8(rx_small[A + 1 : A + 2, :]), 32, 1))
    logp = both(row8(tx_small[A + 2 : A + 3, :]), pltpu.roll(row8(rx_small[A + 2 : A + 3, :]), 32, 1))
    target = rew + discount * (floor - entropy_temp * logp)
    td_gap = q_data - target
    gap_terms = td_gap * td_gap
    mass_terms = both(mass_own, mass_p) - q_data
    dq_data = ((2.0 * td_gap - penalty_weight) * (1.0 / COUNT))[0:1]
    dq_col = jnp.transpose(jnp.broadcast_to(dq_data, (128, 128)))[0:COUNT]
    dq_col = jnp.concatenate([dq_col] * (BLK // 128), axis=1)

    each(1, PLANE, lambda k: ag_copy(k).wait_recv())
    unit = units[...]
    got_sum = spread[...].astype(f32)
    own_rows = [got_sum[16 * r : 16 * r + 8] for r in range(4)]
    other_rows = [got_sum[16 * r + 8 : 16 * r + 16] for r in range(4)]
    rest = jnp.concatenate(own_rows + other_rows, axis=0) - unit
    div_row = jnp.sum(unit * rest, axis=-1, keepdims=True)
    scale = 2.0 * diversity_weight / (COUNT - 1) / COUNT
    norms = jnp.concatenate([norm_own, norm_p], axis=0)
    dgrad = ((scale * rest - unit * (scale * div_row)) / norms).astype(bf16)
    rt[COUNT : 2 * COUNT, :] = dgrad
    tail_x[0:COUNT, :] = dgrad

    def total(row):
        return jnp.sum(jnp.where(lane < COUNT, row, 0.0)[0:1], axis=1, keepdims=True)

    div_sum = jnp.sum(div_row, axis=0, keepdims=True)
    first = lane[0:1]
    stats = jnp.where(first == 0, total(gap_terms), jnp.where(first == 1, total(mass_terms), div_sum))
    stats_out[...] = stats * (1.0 / COUNT)

    def pieces(m):
        at = slice(m * BLK, (m + 1) * BLK)
        far_at = pl.ds(mo(h0 + m * BLK, BLK), BLK)
        h = jnp.concatenate([ho[0:S, far_at], tail_r[COUNT : COUNT + S, at]], axis=0)
        th = jnp.tanh(h)
        a = h * th
        return at, far_at, h, th, a, 0.5 * ((1.0 + th) + (h - a * th)), tail_r[0:COUNT, at]

    for m in range(nb):
        tail_r[:, m * BLK : (m + 1) * BLK] = dot(tail_x[...], w[pl.ds(mo(h0 + m * BLK, BLK), BLK), :], NT)
    for m in range(nb):
        at, far_at, h, th, a, slope, dc = pieces(m)
        gw2[:, far_at] = gw_s[:, at] + jnp.sum(dq_col * (h + a) + dc * slope, axis=0, keepdims=True)
    gw_at = pl.ds(h0, HH)
    cp_gw = far(gw2.at[:, gw_at], gw2.at[:, gw_at], pair_s.at[5], pair_r.at[5], partner)
    cp_gw.start()
    for m in range(nb):
        at, far_at, h, th, a, slope, dc = pieces(m)
        vr = v[:, far_at]
        curve = 0.5 * (1.0 - th * th) * (1.0 - a)
        lt[0:COUNT, at] = (vr * (dq_col * slope + dc * curve)).astype(bf16)
        lt[COUNT : 2 * COUNT, at] = (vr * slope).astype(bf16)
    each(1, PLANE, lambda k: rs_copy(k).wait_send())
    each(1, PLANE, lambda k: ag_copy(k).wait_send())
    for c in x_copies + [cp_obs, cp_small, cp_g, cp_q, cp_qs]:
        c.wait_send()
    cp_gw.wait()
    return None


def run_main(*args):
    vm, dma = pltpu.VMEM, pltpu.SemaphoreType.DMA
    outs = [
        vm((HH, D), f32), vm((2 * COUNT, HH), bf16), vm((2 * COUNT, D), bf16), vm((1, H), f32), vm((1, 128), f32),
    ]
    scratch = [
        vm((NACT, D), bf16), vm((NACT, D), bf16), vm((NACT, D), bf16), vm((H, D), bf16), vm((1, H), f32),
        vm((3, 1, S), jnp.int32), vm((A, S), jnp.int32), vm((2, 1, S), f32),
        vm((2 * S, D), bf16), vm((2 * ROWS, D), bf16), vm((2 * S, D), bf16),
        vm((S, D), bf16), vm((S, D), bf16), vm((24, 128), f32), vm((24, 128), f32),
        vm((HH, 128), f32), vm((2 * S, H), f32), vm((S, D), f32), vm((S, D), f32), vm((1, 128), f32), vm((1, 128), f32),
        vm((COUNT, D), f32), vm((PLANE, 9, 128), f32), vm((PLANE, 9, 128), f32),
        vm((4, 9, 128), f32), vm((16, 128), bf16), vm((COUNT, D), bf16),
        vm((2, BLK, ROWS), f32), vm((HH, 2 * ROWS), bf16), vm((HH, 2 * ROWS), bf16),
        vm((8, 128), f32), vm((8, 128), f32), vm((2 * ROWS, D), bf16), vm((COUNT + S, D), bf16), vm((COUNT + S, HH), f32),
        dma((10,)), dma((NCH,)), dma((6,)), dma((6,)),
        dma((PLANE,)), dma((PLANE,)), dma((4,)), dma((4,)), dma((PLANE,)), dma((PLANE,)),
    ]
    return pl.pallas_call(
        main_kernel,
        out_shape=outs,
        in_specs=[pl.BlockSpec(memory_space=pltpu.HBM)] * len(args),
        out_specs=[pl.BlockSpec(memory_space=pltpu.VMEM)] * len(outs),
        scratch_shapes=scratch,
        compiler_params=pltpu.CompilerParams(collective_id=0, has_side_effects=True, vmem_limit_bytes=40 << 20),
        name="critics",
    )(*(pltpu.with_memory_space_constraint(a, pltpu.HBM) for a in args))


STEP = 256


def weight_kernel(part, lt, rt, gw2_in, stats_in, out, gw2, stats, buf, stats_sc, sems):
    stats_sc[...] = stats_in[:, 0:3]
    copies = [pltpu.make_async_copy(gw2_in, gw2, sems.at[0]), pltpu.make_async_copy(stats_sc, stats, sems.at[1])]
    for c in copies:
        c.start()
    for i in range(HH // STEP):
        r = slice(i * STEP, (i + 1) * STEP)
        buf[r, :] = part[r, :] + dot(lt[:, r], rt[...], TN)
        c = pltpu.make_async_copy(buf.at[pl.ds(i * STEP, STEP)], out.at[0, pl.ds(i * STEP, STEP)], sems.at[2 + i])
        c.start()
        copies.append(c)
    for c in copies:
        c.wait()


def run_weight(*args):
    sds = jax.ShapeDtypeStruct
    hbm = pl.BlockSpec(memory_space=pltpu.HBM)
    return pl.pallas_call(
        weight_kernel,
        out_shape=[sds((1, HH, D), f32), sds((1, H), f32), sds((1, 3), f32)],
        in_specs=[pl.BlockSpec(memory_space=pltpu.VMEM)] * len(args),
        out_specs=[hbm] * 3,
        scratch_shapes=[
            pltpu.VMEM((HH, D), f32), pltpu.VMEM((1, 3), f32), pltpu.SemaphoreType.DMA((2 + HH // STEP,)),
        ],
        compiler_params=pltpu.CompilerParams(vmem_limit_bytes=20 << 20),
        name="weights",
    )(*args)


def body(
    replay_obs, replay_next, batch_rows, data_action, next_action, sampled_actions,
    reward, next_logp, action_table, w1, w2,
):
    row = lambda x: x.reshape(1, S)
    parts = run_main(
        replay_obs, replay_next, row(batch_rows), row(data_action), row(next_action), sampled_actions.T,
        row(reward), row(next_logp), action_table, w1.reshape(H, D), w2,
    )
    return run_weight(*parts)


def solution(mesh):
    finer = Mesh(mesh.devices.reshape(4, 4, 2, 2, mesh.shape["batch"]), (*ENS, "batch"))
    placed = (
        P("batch", None), P("batch", None), P("batch"), P("batch"), P("batch"), P("batch", None),
        P("batch"), P("batch"), P(), P(ENS, None, None), P(ENS, None),
    )
    return jax.shard_map(
        body,
        mesh=finer,
        in_specs=placed,
        out_specs=(P(ENS, "batch", None), P(ENS, None), P(ENS, None)),
        check_vma=False,
    )
```

time: 57.2 us -> 40.1 us (0.70)
  Pallas kernels: 56.3 us -> 39.1 us
    pallas_call x2, Pallas kernels: 56.3 us -> 39.1 us  [the longest x1 35.4 us: run_main(): pl.pallas_call(main_kernel, out_shape=outs, in_specs=[pl.BlockSpec(memory...]
where the time goes in v2:
time: 40.1 us; the launch traced here: 39.9 us
  Pallas kernels  39.1 us (98%)
  between operations  0.8 us (2%)
    pallas_call x1, Pallas kernels, run_main(): pl.pallas_call(main_kernel, out_shape=outs, in_specs=[pl.BlockSpec(memory...  35.4 us
    pallas_call x1, Pallas kernels, run_weight(): pl.pallas_call(weight_kernel, out_shape=[sds((1, HH, D), f32), sds((1, H)...  3.71 us

profile of v2, /device:TPU:0, one launch (start us, length us, event | category | flops | bytes accessed | tf_op | source)
XLA Modules:
  0.0 39.9 jit_solution(8614975780289057629)
XLA Ops:
  0.6 35.4 %critics.1 = (f32[2048,1024]{1,0:T(8,128)S(1)}, bf16[128,2048]{1,0:T(8,128)(2,1)S(1)}, bf16[128,1024]{1,0:T(8,128)(2,1)S(1)}, f32[1,4096]{1,0:T(1,128)S(1)}, f32[1,128]{1,0:T(1,128)S(1)}) custom-call(bf16[256,1024]{1,0:T(8,128)(2,1)} %obs_hbm.1, bf16[256,1024]{1,0:T(8,128)(2,1)} %next_hbm.1, s32[1,32]{1,0:T(1,128)} %bitcast.9, s32[1,32]{1,0:T(1,128)} %bitcast.10, ...), custom_call_target="tpu_custom_call" | custom-call | tf_op jit(solution)/shard_map/critics/pallas_call | solution.py:408
  36.0 3.7 %weights.1 = (f32[1,2048,1024]{2,1,0:T(8,128)}, f32[1,4096]{1,0:T(1,128)}, f32[1,3]{1,0:T(1,128)}) custom-call(f32[2048,1024]{1,0:T(8,128)S(1)} %get-tuple-element.8.part, bf16[128,2048]{1,0:T(8,128)(2,1)S(1)} %get-tuple-element.9.lt, bf16[128,1024]{1,0:T(8,128)(2,1)S(1)} %get-tuple-element.10.rt, f32[1,4096]{1,0:T(1,128)S(1)} %get-tuple-element.11.gw2_in, ...), custom_call_target="tpu_custom_call" | custom-call | tf_op jit(solution)/shard_map/weights/pallas_call | solution.py:440

commit v3 on v2

v3 whole, which is shorter than its diff:
```python
import jax
import jax.numpy as jnp
from jax import lax
from jax.experimental import pallas as pl
from jax.experimental.pallas import tpu as pltpu
from jax.sharding import Mesh
from jax.sharding import PartitionSpec as P

ENS = ("ens_0", "ens_1", "ens_2", "ens_3")
MESH_ID = pl.DeviceIdType.MESH
f32, bf16 = jnp.float32, jnp.bfloat16

D, H, HH = 1024, 4096, 2048
S, A, NACT = 32, 16, 256
ROWS = S * A
CH = 512
NCH = H // CH
BLK = 512
SUB = 32
PLANE = 32
COUNT = 64
discount, entropy_temp, penalty_weight, diversity_weight = 0.99, 0.2, 1.0, 1000.0

NN = (((1,), (0,)), ((), ()))
NT = (((1,), (1,)), ((), ()))
TN = (((0,), (0,)), ((), ()))


def dot(a, b, dims=NN):
    return lax.dot_general(a, b, dims, preferred_element_type=f32)


def mo(x, m):
    return pl.multiple_of(x, m)


def each(lo, hi, fn):
    def step(k, carry):
        fn(k)
        return carry

    lax.fori_loop(lo, hi, step, 0)


def iota(shape, dim):
    return lax.broadcasted_iota(jnp.int32, shape, dim)


def row8(x):
    return jnp.broadcast_to(x, (8, 128))


def main_kernel(
    obs_hbm, next_hbm, rows_hbm, dact_hbm, nact_hbm, sact_hbm, rew_hbm, logp_hbm, table_hbm, w_hbm, v_hbm,
    part, w, rt, tail_x, ho, v, gw2, dq_out, stats_out,
    tab_obs, tab_next, table, ids, sact, rl,
    xdn, xs, xd, tx_obs, rx_obs, tx_small, rx_small,
    vcol, h_next, gin, rx_g, tx_q, rx_q, units, rs_tx, rs_buf, xr, ag_tx, spread,
    h_buf, sl, silu, q_own_sc, q_far_sc, rx_q_own, rx_q_far, x_out, gw_part,
    in_sem, w_sem, pair_s, pair_r, x_s, x_r, many,
):
    z, y, xh, core = (lax.axis_index(n) for n in ENS)
    b = lax.axis_index("batch")
    me = z * 8 + y * 2 + core
    xpos = xh * 2 + b

    zs = [lax.rem(z + d, 4) for d in range(4)]
    ys = [lax.rem(y + d, 4) for d in range(4)]
    cores = [core, 1 - core]
    order = sorted(range(1, PLANE), key=lambda k: -((0, 1, 2, 1)[k // 8] + (0, 1, 2, 1)[k // 2 % 4]))

    def plane(k):
        pz, py, pc = zs[k // 8], ys[k // 2 % 4], cores[k % 2]
        return pz * 8 + py * 2 + pc, (pz, py, xh, pc, b)

    def line(d):
        p = lax.rem(xpos + d, 4)
        return (z, y, lax.div(p, 2), core, lax.rem(p, 2))

    partner = (z, y, xh, core, 1 - b)
    h0 = mo(b * HH, HH)

    def far(src, dst, ssem, rsem, device):
        return pltpu.make_async_remote_copy(
            src_ref=src, dst_ref=dst, send_sem=ssem, recv_sem=rsem, device_id=device, device_id_type=MESH_ID
        )

    loads = [
        pltpu.make_async_copy(src, dst, in_sem.at[i])
        for i, (src, dst) in enumerate(
            [
                (rows_hbm, ids.at[0]), (dact_hbm, ids.at[1]), (nact_hbm, ids.at[2]), (sact_hbm, sact),
                (rew_hbm, rl.at[0]), (logp_hbm, rl.at[1]),
                (obs_hbm, tab_obs), (table_hbm, table), (next_hbm, tab_next), (v_hbm, v),
            ]
        )
    ]
    for c in loads:
        c.start()

    def w_copy(c):
        at = pl.ds(c * CH, CH)
        return pltpu.make_async_copy(w_hbm.at[at], w.at[at], w_sem.at[c])

    barrier = pltpu.get_barrier_semaphore()

    def greet(device):
        pl.semaphore_signal(barrier, inc=1, device_id=device, device_id_type=MESH_ID)

    for k in order:
        greet(plane(k)[1])
    for d in (1, 2, 3):
        greet(line(d))
    for c in range(4):
        w_copy(c).start()

    for c in loads[:6]:
        c.wait()

    lanes = iota((S, NACT), 1).astype(f32)
    eye = iota((S, S), 0) == iota((S, S), 1)
    ones = jnp.ones((S, NACT), bf16)

    def one_hot(row, value):
        diag = jnp.where(eye, jnp.broadcast_to(row, (S, S)), 0.0).astype(bf16)
        return jnp.where(dot(diag, ones) == lanes, value, 0.0).astype(bf16)

    def sample_hot(sact_f):
        pick = jnp.where((iota((ROWS, S), 0) & (S - 1)) == iota((ROWS, S), 1), 1.0, 0.0).astype(bf16)
        each_sample = dot(pick, sact_f.astype(bf16), NT)
        mine = lax.shift_right_logical(iota((ROWS, A), 0), 5) == iota((ROWS, A), 1)
        index = dot(jnp.where(mine, each_sample, 0.0).astype(bf16), jnp.ones((A, NACT), bf16))
        return jnp.where(index == iota((ROWS, NACT), 1).astype(f32), 0.5, 0.0).astype(bf16)

    rows_oh, dact_oh, nact_oh = (one_hot(ids[i].astype(f32), 0.5) for i in range(3))
    own_hot = sample_hot(sact[...].astype(f32))
    tx_small[...] = jnp.zeros_like(tx_small)
    tx_small[0:A, 0:S] = sact[...].astype(f32)
    tx_small[A : A + 1, 0:S] = ids[1].astype(f32)
    tx_small[A + 1 : A + 2, 0:S] = rl[0]
    tx_small[A + 2 : A + 3, 0:S] = rl[1]
    for c in loads[6:]:
        c.wait()
    for c in range(4, NCH):
        w_copy(c).start()

    obs = dot(rows_oh, tab_obs[...])
    nxt = dot(rows_oh, tab_next[...])
    tx_obs[...] = obs.astype(bf16)
    half_data = (obs + dot(dact_oh, table[...])).astype(bf16)
    xdn[0:S, :] = half_data
    xdn[S : 2 * S, :] = (nxt + dot(nact_oh, table[...])).astype(bf16)
    xd[0:S, :] = half_data

    def own_act(c, q_acc):
        at = slice(c * CH, (c + 1) * CH)
        h = jnp.concatenate([ho[:, at], h_next[c % 2]], axis=0)
        th = jnp.tanh(h)
        p = 1.0 + th
        so = h * p
        vr = v[:, at]
        sv = so * vr
        for k in range(CH // 128):
            q_acc = q_acc + sv[:, k * 128 : (k + 1) * 128]
        co = (0.5 * vr * (p[0:S] + so[0:S] * (1.0 - th[0:S]))).astype(bf16)
        g = dot(co, w[at, :])
        gin[...] = g if c == 0 else gin[...] + g
        return q_acc

    def spread_v(i):
        at = pl.ds(mo(h0 + i * 128, 128), 128)
        vcol[i * 128 : (i + 1) * 128, :] = jnp.transpose(jnp.broadcast_to(0.5 * v[:, at], (128, 128)))

    q_acc = jnp.zeros((2 * S, 128), f32)
    cp_obs = far(tx_obs, rx_obs, pair_s.at[0], pair_r.at[0], partner)
    cp_small = far(tx_small, rx_small, pair_s.at[1], pair_r.at[1], partner)
    for c in range(NCH):
        if c % 2 == 0:
            w_copy(c).wait()
            w_copy(c + 1).wait()
        h = dot(xdn[...], w[c * CH : (c + 1) * CH, :], NT)
        ho[:, c * CH : (c + 1) * CH] = h[0:S]
        h_next[c % 2] = h[S : 2 * S]
        if c > 0:
            q_acc = own_act(c - 1, q_acc)
        for i in range(2):
            spread_v(2 * c + i)
    q_acc = own_act(NCH - 1, q_acc)
    q_own = jnp.sum(jnp.transpose(jnp.concatenate([q_acc, jnp.zeros((64, 128), f32)], axis=0)), axis=0, keepdims=True)
    tx_q[...] = q_own

    def norm_of(g):
        return jnp.sqrt(jnp.sum(g * g, axis=-1, keepdims=True) + 1.0)

    g_own = gin[...]
    norm_own = norm_of(g_own)
    u_own = g_own / norm_own
    units[0:S, :] = u_own
    q_hi = q_own.astype(bf16).astype(f32)
    q_mid = (q_own - q_hi).astype(bf16).astype(f32)
    q_rows = jnp.concatenate([q_hi, q_mid, q_own - q_hi - q_mid, jnp.zeros((5, 128), f32)], axis=0)
    for j in range(PLANE):
        r, c = j // 8, j % 8
        u_tile = u_own[8 * r : 8 * r + 8, 128 * c : 128 * c + 128]
        rs_tx[j] = jnp.concatenate([u_tile, q_rows], axis=0).astype(bf16)

    def rs_copy(k):
        j, device = plane(k)
        return far(rs_tx.at[j], rs_buf.at[k], many.at[0], many.at[1], device)

    all_in = rs_buf.at[pl.ds(1, PLANE - 1)]
    rs_all = far(all_in, all_in, many.at[0], many.at[1], partner)
    pl.semaphore_wait(barrier, PLANE - 1 + 3)
    for k in order:
        rs_copy(k).start()
    cp_obs.start()
    cp_small.start()
    cp_g = far(gin, rx_g, pair_s.at[2], pair_r.at[2], partner)
    cp_q = far(tx_q, rx_q, pair_s.at[3], pair_r.at[3], partner)
    cp_g.start()
    cp_q.start()

    def build(hot, base, off):
        for p in range(2):
            h_buf[p] = dot(hot, table[:, p * 512 : (p + 1) * 512])
        for i in range(A):
            for p in range(2):
                x = (base[:, p * 512 : (p + 1) * 512] + h_buf[p, i * S : (i + 1) * S, :]).astype(bf16)
                xs[off + i * S : off + (i + 1) * S, p * 512 : (p + 1) * 512] = x

    nb = HH // BLK

    def product(n):
        half, m = divmod(n, nb)
        h_buf[m] = dot(w[pl.ds(mo(h0 + m * BLK, BLK), BLK), :], xs[half * ROWS : (half + 1) * ROWS, :], NT)

    def activate(n, q):
        half, m = divmod(n, nb)
        at = slice(half * ROWS, (half + 1) * ROWS)
        for i in range(BLK // SUB):
            h = h_buf[m, i * SUB : (i + 1) * SUB, :]
            r = slice(m * BLK + i * SUB, m * BLK + (i + 1) * SUB)
            th = jnp.tanh(h)
            p = 1.0 + th
            so = h * p
            vh = vcol[r, :]
            vh = jnp.concatenate([vh, vh, vh, vh], axis=1)
            silu[r, at] = so.astype(bf16)
            sl[r, at] = (vh * (p + so * (1.0 - th))).astype(bf16)
            sv = so * vh
            q = q + ((sv[0:8] + sv[8:16]) + (sv[16:24] + sv[24:32]))
        return q

    def keep_q(q, ref):
        q = 2.0 * jnp.sum(q, axis=0, keepdims=True)
        for k in range(4):
            ref[k : k + 1, :] = q[:, k * 128 : (k + 1) * 128]

    q_zero = jnp.zeros((8, ROWS), f32)
    cp_q_own = far(q_own_sc, rx_q_own, pair_s.at[4], pair_r.at[4], partner)
    cp_q_far = far(q_far_sc, rx_q_far, pair_s.at[5], pair_r.at[5], partner)
    x_copies = [far(xr.at[0], xr.at[d], x_s.at[d - 1], x_r.at[d - 1], line(d)) for d in (1, 2, 3)]

    build(own_hot, obs, 0)
    product(0)
    q = q_zero
    for n in range(1, nb):
        product(n)
        q = activate(n - 1, q)

    cp_obs.wait_recv()
    cp_small.wait_recv()
    obs_p = rx_obs[...].astype(f32)
    build(sample_hot(rx_small[0:A, 0:S]), obs_p, ROWS)
    half_p = (obs_p + dot(one_hot(rx_small[A : A + 1, 0:S], 0.5), table[...])).astype(bf16)
    xd[S : 2 * S, :] = half_p
    tail_x[COUNT : COUNT + S, :] = half_p
    product(nb)
    keep_q(activate(nb - 1, q), q_own_sc)

    rs_all.wait_recv()
    rs_buf[0] = rs_tx[me]
    got = rs_buf[...].astype(f32)
    xr[0, 0:8, :] = jnp.sum(got[:, 0:8, :], axis=0)
    xr[0, 8:9, :] = jnp.min((got[:, 8:9, :] + got[:, 9:10, :]) + got[:, 10:11, :], axis=0)
    for c in x_copies:
        c.start()
    cp_q_own.start()
    q = q_zero
    for n in range(nb + 1, 2 * nb):
        product(n)
        q = activate(n - 1, q)

    keep_q(activate(2 * nb - 1, q), q_far_sc)
    cp_q_far.start()

    for c in x_copies:
        c.wait_recv()
    row_me = mo(lax.div(me, 8) * 16, 16)
    col_me = mo(lax.rem(me, 8) * 128, 128)
    ag_tx[...] = jnp.concatenate([xr[0, 0:8, :] + xr[2, 0:8, :], xr[1, 0:8, :] + xr[3, 0:8, :]], axis=0).astype(bf16)

    def ag_copy(k):
        dst = spread.at[pl.ds(row_me, 16), pl.ds(col_me, 128)]
        return far(ag_tx, dst, many.at[2], many.at[3], plane(k)[1])

    ag_all = far(all_in, all_in, many.at[2], many.at[3], partner)

    for k in order:
        ag_copy(k).start()
    spread[pl.ds(row_me, 16), pl.ds(col_me, 128)] = ag_tx[...]

    cp_g.wait_recv()
    g_p = rx_g[...]
    norm_p = norm_of(g_p)
    units[S : 2 * S, :] = g_p / norm_p
    rt[0:COUNT, :] = (xd[...].astype(f32) * 2.0).astype(bf16)

    def penalty(q4, half):
        m = row8(jnp.sum(jnp.exp(q4), axis=0, keepdims=True))
        m = m + pltpu.roll(m, 32, 1)
        mass = jnp.log(m + pltpu.roll(m, 64, 1))
        dq = jnp.exp(q4 - mass[0:4]) * (penalty_weight / COUNT)
        for r in range(4):
            col = jnp.transpose(jnp.broadcast_to(dq[r : r + 1, :], (128, 128))) * 2.0
            rows = slice(half * ROWS + r * 128, half * ROWS + (r + 1) * 128)
            for c in range(8):
                at = slice(c * 128, (c + 1) * 128)
                x_out[rows, at] = (xs[rows, at].astype(f32) * col).astype(bf16)
        return mass, dq

    def weight_part(m, half, first):
        at = slice(half * ROWS, (half + 1) * ROWS)
        r = slice(m * BLK, (m + 1) * BLK)
        g = dot(sl[r, at], x_out[at, :])
        part[r, :] = g if first else part[r, :] + g

    def readout_part(m, dq, half, first):
        for i in range(BLK // SUB):
            r = slice(m * BLK + i * SUB, m * BLK + (i + 1) * SUB)
            acc = None if first else gw_part[r, :]
            for k in range(4):
                c = slice(half * ROWS + k * 128, half * ROWS + (k + 1) * 128)
                term = silu[r, c].astype(f32) * dq[k : k + 1, :]
                acc = term if acc is None else acc + term
            gw_part[r, :] = acc
        if not first:
            for k in range(BLK // 128):
                rows = slice(m * BLK + k * 128, m * BLK + (k + 1) * 128)
                dst = pl.ds(mo(h0 + m * BLK + k * 128, 128), 128)
                gw2[:, dst] = jnp.sum(jnp.transpose(gw_part[rows, :]), axis=0, keepdims=True)

    cp_q_own.wait_recv()
    mass_p, dq_p = penalty(q_far_sc[...] + rx_q_own[...], 1)

    for m in range(nb):
        weight_part(m, 1, True)
        readout_part(m, dq_p, 1, True)
    cp_q_far.wait_recv()
    mass_own, dq_own = penalty(q_own_sc[...] + rx_q_far[...], 0)
    for m in range(nb):
        if m < 2:
            weight_part(m, 0, False)
        readout_part(m, dq_own, 0, False)
    gw_at = pl.ds(h0, HH)
    cp_gw = far(gw2.at[:, gw_at], gw2.at[:, gw_at], pair_s.at[6], pair_r.at[6], partner)
    cp_gw.start()
    for m in range(2, nb):
        weight_part(m, 0, False)

    cp_q.wait_recv()
    lane = iota((8, 128), 1)
    left = lane < S

    def both(own, other):
        return jnp.where(left, own, other)

    floor_own, floor_p = jnp.minimum(xr[0, 8:9, :], xr[2, 8:9, :]), jnp.minimum(xr[1, 8:9, :], xr[3, 8:9, :])
    floor = both(pltpu.roll(row8(floor_own), 96, 1), row8(floor_p))
    q_data = both(row8(tx_q[...]), pltpu.roll(row8(rx_q[...]), 32, 1))
    rew = both(row8(tx_small[A + 1 : A + 2, :]), pltpu.roll(row8(rx_small[A + 1 : A + 2, :]), 32, 1))
    logp = both(row8(tx_small[A + 2 : A + 3, :]), pltpu.roll(row8(rx_small[A + 2 : A + 3, :]), 32, 1))
    target = rew + discount * (floor - entropy_temp * logp)
    td_gap = q_data - target
    gap_terms = td_gap * td_gap
    mass_terms = both(mass_own, mass_p) - q_data
    dq_data = ((2.0 * td_gap - penalty_weight) * (1.0 / COUNT))[0:1]
    dq_out[...] = jnp.transpose(jnp.broadcast_to(dq_data, (128, 128)))[0:COUNT]

    ag_all.wait_recv()
    unit = units[...]
    got_sum = spread[...].astype(f32)
    own_rows = [got_sum[16 * r : 16 * r + 8] for r in range(4)]
    other_rows = [got_sum[16 * r + 8 : 16 * r + 16] for r in range(4)]
    rest = jnp.concatenate(own_rows + other_rows, axis=0) - unit
    div_row = jnp.sum(unit * rest, axis=-1, keepdims=True)
    scale = 2.0 * diversity_weight / (COUNT - 1) / COUNT
    norms = jnp.concatenate([norm_own, norm_p], axis=0)
    dgrad = ((scale * rest - unit * (scale * div_row)) / norms).astype(bf16)
    rt[COUNT : 2 * COUNT, :] = dgrad
    tail_x[0:COUNT, :] = dgrad

    def total(row):
        return jnp.sum(jnp.where(lane < COUNT, row, 0.0)[0:1], axis=1, keepdims=True)

    div_sum = jnp.sum(div_row, axis=0, keepdims=True)
    first = lane[0:1]
    stats = jnp.where(first == 0, total(gap_terms), jnp.where(first == 1, total(mass_terms), div_sum))
    stats_out[...] = stats * (1.0 / COUNT)

    rs_all.wait_send()
    ag_all.wait_send()
    for c in x_copies + [cp_obs, cp_small, cp_g, cp_q, cp_q_own, cp_q_far]:
        c.wait_send()
    cp_gw.wait()
    return None


def run_main(*args):
    vm, dma = pltpu.VMEM, pltpu.SemaphoreType.DMA
    outs = [
        vm((HH, D), f32), vm((H, D), bf16), vm((2 * COUNT, D), bf16), vm((COUNT + S, D), bf16), vm((S, H), f32),
        vm((1, H), f32), vm((1, H), f32), vm((COUNT, 128), f32), vm((1, 128), f32),
    ]
    scratch = [
        vm((NACT, D), bf16), vm((NACT, D), bf16), vm((NACT, D), bf16),
        vm((3, 1, S), jnp.int32), vm((A, S), jnp.int32), vm((2, 1, S), f32),
        vm((2 * S, D), bf16), vm((2 * ROWS, D), bf16), vm((2 * S, D), bf16),
        vm((S, D), bf16), vm((S, D), bf16), vm((24, 128), f32), vm((24, 128), f32),
        vm((HH, 128), f32), vm((2, S, CH), f32), vm((S, D), f32), vm((S, D), f32), vm((1, 128), f32), vm((1, 128), f32),
        vm((COUNT, D), f32), vm((PLANE, 16, 128), bf16), vm((PLANE, 16, 128), bf16),
        vm((4, 9, 128), f32), vm((16, 128), bf16), vm((COUNT, D), bf16),
        vm((HH // BLK, BLK, ROWS), f32), vm((HH, 2 * ROWS), bf16), vm((HH, 2 * ROWS), bf16),
        vm((4, 128), f32), vm((4, 128), f32), vm((4, 128), f32), vm((4, 128), f32),
        vm((2 * ROWS, D), bf16), vm((HH, 128), f32),
        dma((10,)), dma((NCH,)), dma((7,)), dma((7,)),
        dma((3,)), dma((3,)), dma((4,)),
    ]
    return pl.pallas_call(
        main_kernel,
        out_shape=outs,
        in_specs=[pl.BlockSpec(memory_space=pltpu.HBM)] * len(args),
        out_specs=[pl.BlockSpec(memory_space=pltpu.VMEM)] * len(outs),
        scratch_shapes=scratch,
        compiler_params=pltpu.CompilerParams(collective_id=0, has_side_effects=True, vmem_limit_bytes=36 << 20),
        name="critics",
    )(*(pltpu.with_memory_space_constraint(a, pltpu.HBM) for a in args))


STEP = 256


def weight_kernel(
    part, w, rt, tail_x, ho, v, gw_in, dq_in, stats_in, out, gw2, stats, buf, lt, gw_sc, stats_sc, sems
):
    b = lax.axis_index("batch")
    stats_sc[...] = stats_in[:, 0:3]
    copies = [pltpu.make_async_copy(stats_sc, stats, sems.at[0])]
    copies[0].start()
    dq = jnp.concatenate([dq_in[...]] * (STEP // 128), axis=1)

    def terms(at):
        r = dot(tail_x[...], w[at, :], NT)
        h = jnp.concatenate([ho[:, at], r[COUNT : COUNT + S]], axis=0)
        dc = r[0:COUNT]
        th = jnp.tanh(h)
        p = 1.0 + th
        so = h * p
        slope = 0.5 * (p + so * (1.0 - th))
        gw_sc[:, at] = gw_in[:, at] + jnp.sum(dq * so + dc * slope, axis=0, keepdims=True)
        return h, th, p, slope, dc

    def near(m):
        return pl.ds(mo(b * HH + m * STEP, STEP), STEP)

    def back(m, h, th, p, slope, dc):
        vr = v[:, near(m)]
        curve = 0.5 * (p * (1.0 - th)) * (1.0 - h * th)
        lt[0:COUNT, m * STEP : (m + 1) * STEP] = (vr * (dq * slope + dc * curve)).astype(bf16)
        lt[COUNT : 2 * COUNT, m * STEP : (m + 1) * STEP] = (vr * slope).astype(bf16)

    last = HH // STEP
    own_next = {0: [1], 1: [2], 2: [3], 3: [4, 5], 4: [6, 7]}
    other_next = {4: [0, 1], 5: [2, 3, 4, 5, 6, 7]}
    back(0, *terms(near(0)))
    for m in range(last):
        r = slice(m * STEP, (m + 1) * STEP)
        buf[r, :] = part[r, :] + dot(lt[:, r], rt[...], TN)
        for k in own_next.get(m, []):
            back(k, *terms(near(k)))
        c = pltpu.make_async_copy(buf.at[pl.ds(m * STEP, STEP)], out.at[0, pl.ds(m * STEP, STEP)], sems.at[2 + m])
        c.start()
        copies.append(c)
        for k in other_next.get(m, []):
            terms(pl.ds(mo((1 - b) * HH + k * STEP, STEP), STEP))
        if m == 5:
            copies.append(pltpu.make_async_copy(gw_sc, gw2, sems.at[1]))
            copies[-1].start()
    for c in copies:
        c.wait()
    return None


def run_weight(*args):
    sds = jax.ShapeDtypeStruct
    hbm = pl.BlockSpec(memory_space=pltpu.HBM)
    vm = pltpu.VMEM
    return pl.pallas_call(
        weight_kernel,
        out_shape=[sds((1, HH, D), f32), sds((1, H), f32), sds((1, 3), f32)],
        in_specs=[pl.BlockSpec(memory_space=vm)] * len(args),
        out_specs=[hbm] * 3,
        scratch_shapes=[
            vm((HH, D), f32), vm((2 * COUNT, HH), bf16), vm((1, H), f32), vm((1, 3), f32),
            pltpu.SemaphoreType.DMA((2 + HH // STEP,)),
        ],
        compiler_params=pltpu.CompilerParams(vmem_limit_bytes=20 << 20),
        name="weights",
    )(*args)


def body(
    replay_obs, replay_next, batch_rows, data_action, next_action, sampled_actions,
    reward, next_logp, action_table, w1, w2,
):
    row = lambda x: x.reshape(1, S)
    parts = run_main(
        replay_obs, replay_next, row(batch_rows), row(data_action), row(next_action), sampled_actions.T,
        row(reward), row(next_logp), action_table, w1.reshape(H, D), w2,
    )
    return run_weight(*parts)


def solution(mesh):
    finer = Mesh(mesh.devices.reshape(4, 4, 2, 2, mesh.shape["batch"]), (*ENS, "batch"))
    placed = (
        P("batch", None), P("batch", None), P("batch"), P("batch"), P("batch"), P("batch", None),
        P("batch"), P("batch"), P(), P(ENS, None, None), P(ENS, None),
    )
    return jax.shard_map(
        body,
        mesh=finer,
        in_specs=placed,
        out_specs=(P(ENS, "batch", None), P(ENS, None), P(ENS, None)),
        check_vma=False,
    )
```

time: 40.1 us -> 34.3 us (0.86)
  Pallas kernels: 39.1 us -> 33.3 us
    pallas_call x1, Pallas kernels: 35.4 us -> 27.5 us  [run_main(): pl.pallas_call(main_kernel, out_shape=outs, in_specs=[pl.BlockSpec(memory...]
    pallas_call x1, Pallas kernels: 3.71 us -> 5.84 us  [run_weight(): pl.pallas_call(weight_kernel, out_shape=[sds((1, HH, D), f32), sds((1, H)...]
where the time goes in v3:
time: 34.3 us; the launch traced here: 34.1 us
  Pallas kernels  33.3 us (97%)
  between operations  0.8 us (2%)
    pallas_call x1, Pallas kernels, run_main(): pl.pallas_call(main_kernel, out_shape=outs, in_specs=[pl.BlockSpec(memory...  27.5 us
    pallas_call x1, Pallas kernels, run_weight(): pl.pallas_call(weight_kernel, out_shape=[sds((1, HH, D), f32), sds((1, H)...  5.84 us

profile of v3, /device:TPU:0, one launch (start us, length us, event | category | flops | bytes accessed | tf_op | source)
XLA Modules:
  0.0 34.1 jit_solution(9270458896448539394)
XLA Ops:
  0.6 27.5 %critics.1 = (f32[2048,1024]{1,0:T(8,128)S(1)}, bf16[4096,1024]{1,0:T(8,128)(2,1)S(1)}, bf16[128,1024]{1,0:T(8,128)(2,1)S(1)}, bf16[96,1024]{1,0:T(8,128)(2,1)S(...) custom-call(bf16[256,1024]{1,0:T(8,128)(2,1)} %obs_hbm.1, ...), custom_call_target="tpu_custom_call" | custom-call | tf_op jit(solution)/shard_map/critics/pallas_call | solution.py:439
  28.1 5.8 %weights.1 = (f32[1,2048,1024]{2,1,0:T(8,128)}, f32[1,4096]{1,0:T(1,128)}, f32[1,3]{1,0:T(1,128)}) custom-call(f32[2048,1024]{1,0:T(8,128)S(1)} %get-tuple-element.12.part, bf16[4096,1024]{1,0:T(8,128)(2,1)S(1)} %get-tuple-element.13.w, bf16[128,1024]{1,0:T(8,128)(2,1)S(1)} %get-tuple-element.14.rt, bf16[96,1024]{1,0:T(8,128)(2,1)S(1)} %get-tuple-element.15.tail_x, ...), custom_call_target="tpu_custom_call" | custom-call | tf_op jit(solution)/shard_map/weights/pallas_call | solution.py:508

commit v4 on v3

--- a/solution.py
+++ b/solution.py
@@ -52,8 +52,8 @@
 
 def main_kernel(
     obs_hbm, next_hbm, rows_hbm, dact_hbm, nact_hbm, sact_hbm, rew_hbm, logp_hbm, table_hbm, w_hbm, v_hbm,
-    part, w, rt, tail_x, ho, v, gw2, dq_out, stats_out,
-    tab_obs, tab_next, table, ids, sact, rl,
+    part, wt, rt, tail_x, ho, v, gw2, dq_out, stats_out,
+    w, tab_obs, tab_next, table, ids, sact, rl,
     xdn, xs, xd, tx_obs, rx_obs, tx_small, rx_small,
     vcol, h_next, gin, rx_g, tx_q, rx_q, units, rs_tx, rs_buf, xr, ag_tx, spread,
     h_buf, sl, silu, q_own_sc, q_far_sc, rx_q_own, rx_q_far, x_out, gw_part,
@@ -334,6 +334,8 @@
         r = slice(m * BLK, (m + 1) * BLK)
         g = dot(sl[r, at], x_out[at, :])
         part[r, :] = g if first else part[r, :] + g
+        r = slice((half * nb + m) * BLK, (half * nb + m + 1) * BLK)
+        wt[:, r] = jnp.transpose(w[r, :])
 
     def readout_part(m, dq, half, first):
         for i in range(BLK // SUB):
@@ -419,11 +421,11 @@
 def run_main(*args):
     vm, dma = pltpu.VMEM, pltpu.SemaphoreType.DMA
     outs = [
-        vm((HH, D), f32), vm((H, D), bf16), vm((2 * COUNT, D), bf16), vm((COUNT + S, D), bf16), vm((S, H), f32),
+        vm((HH, D), f32), vm((D, H), bf16), vm((2 * COUNT, D), bf16), vm((COUNT + S, D), bf16), vm((S, H), f32),
         vm((1, H), f32), vm((1, H), f32), vm((COUNT, 128), f32), vm((1, 128), f32),
     ]
     scratch = [
-        vm((NACT, D), bf16), vm((NACT, D), bf16), vm((NACT, D), bf16),
+        vm((H, D), bf16), vm((NACT, D), bf16), vm((NACT, D), bf16), vm((NACT, D), bf16),
         vm((3, 1, S), jnp.int32), vm((A, S), jnp.int32), vm((2, 1, S), f32),
         vm((2 * S, D), bf16), vm((2 * ROWS, D), bf16), vm((2 * S, D), bf16),
         vm((S, D), bf16), vm((S, D), bf16), vm((24, 128), f32), vm((24, 128), f32),
@@ -447,20 +449,18 @@
     )(*(pltpu.with_memory_space_constraint(a, pltpu.HBM) for a in args))
 
 
-STEP = 256
-
-
 def weight_kernel(
-    part, w, rt, tail_x, ho, v, gw_in, dq_in, stats_in, out, gw2, stats, buf, lt, gw_sc, stats_sc, sems
+    part, wt, rt, tail_x, ho, v, gw_in, dq_in, stats_in, out, gw2, stats, buf, lt, gw_sc, stats_sc, sems
 ):
     b = lax.axis_index("batch")
     stats_sc[...] = stats_in[:, 0:3]
     copies = [pltpu.make_async_copy(stats_sc, stats, sems.at[0])]
     copies[0].start()
-    dq = jnp.concatenate([dq_in[...]] * (STEP // 128), axis=1)
-
-    def terms(at):
-        r = dot(tail_x[...], w[at, :], NT)
+
+    def terms(start, size):
+        at = pl.ds(mo(start, 256), size)
+        dq = jnp.concatenate([dq_in[...]] * (size // 128), axis=1)
+        r = dot(tail_x[...], wt[:, at])
         h = jnp.concatenate([ho[:, at], r[COUNT : COUNT + S]], axis=0)
         dc = r[0:COUNT]
         th = jnp.tanh(h)
@@ -468,34 +468,29 @@
         so = h * p
         slope = 0.5 * (p + so * (1.0 - th))
         gw_sc[:, at] = gw_in[:, at] + jnp.sum(dq * so + dc * slope, axis=0, keepdims=True)
-        return h, th, p, slope, dc
-
-    def near(m):
-        return pl.ds(mo(b * HH + m * STEP, STEP), STEP)
-
-    def back(m, h, th, p, slope, dc):
-        vr = v[:, near(m)]
+        return at, dq, h, th, p, slope, dc
+
+    def back(start, size):
+        at, dq, h, th, p, slope, dc = terms(b * HH + start, size)
+        vr = v[:, at]
         curve = 0.5 * (p * (1.0 - th)) * (1.0 - h * th)
-        lt[0:COUNT, m * STEP : (m + 1) * STEP] = (vr * (dq * slope + dc * curve)).astype(bf16)
-        lt[COUNT : 2 * COUNT, m * STEP : (m + 1) * STEP] = (vr * slope).astype(bf16)
-
-    last = HH // STEP
-    own_next = {0: [1], 1: [2], 2: [3], 3: [4, 5], 4: [6, 7]}
-    other_next = {4: [0, 1], 5: [2, 3, 4, 5, 6, 7]}
-    back(0, *terms(near(0)))
-    for m in range(last):
-        r = slice(m * STEP, (m + 1) * STEP)
+        lt[0:COUNT, start : start + size] = (vr * (dq * slope + dc * curve)).astype(bf16)
+        lt[COUNT : 2 * COUNT, start : start + size] = (vr * slope).astype(bf16)
+
+    blocks = ((0, 256), (256, 256), (512, 512), (1024, 512), (1536, 512))
+    back(*blocks[0])
+    for m, (start, size) in enumerate(blocks):
+        r = slice(start, start + size)
         buf[r, :] = part[r, :] + dot(lt[:, r], rt[...], TN)
-        for k in own_next.get(m, []):
-            back(k, *terms(near(k)))
-        c = pltpu.make_async_copy(buf.at[pl.ds(m * STEP, STEP)], out.at[0, pl.ds(m * STEP, STEP)], sems.at[2 + m])
-        c.start()
-        copies.append(c)
-        for k in other_next.get(m, []):
-            terms(pl.ds(mo((1 - b) * HH + k * STEP, STEP), STEP))
-        if m == 5:
-            copies.append(pltpu.make_async_copy(gw_sc, gw2, sems.at[1]))
-            copies[-1].start()
+        if m + 1 < len(blocks):
+            back(*blocks[m + 1])
+        at = pl.ds(start, size)
+        copies.append(pltpu.make_async_copy(buf.at[at], out.at[0, at], sems.at[2 + m]))
+        copies[-1].start()
+    for m in range(HH // BLK):
+        terms((1 - b) * HH + m * BLK, BLK)
+    copies.append(pltpu.make_async_copy(gw_sc, gw2, sems.at[1]))
+    copies[-1].start()
     for c in copies:
         c.wait()
     return None
@@ -512,7 +507,7 @@
         out_specs=[hbm] * 3,
         scratch_shapes=[
             vm((HH, D), f32), vm((2 * COUNT, HH), bf16), vm((1, H), f32), vm((1, 3), f32),
-            pltpu.SemaphoreType.DMA((2 + HH // STEP,)),
+            pltpu.SemaphoreType.DMA((7,)),
         ],
         compiler_params=pltpu.CompilerParams(vmem_limit_bytes=20 << 20),
         name="weights",

time: 34.3 us -> 33.7 us (0.983)
  Pallas kernels: 33.3 us -> 32.8 us
    pallas_call x1, Pallas kernels: 5.84 us -> 5.07 us  [run_weight(): pl.pallas_call(weight_kernel, out_shape=[sds((1, HH, D), f32), sds((1, H)...]
where the time goes in v4:
time: 33.7 us; the launch traced here: 33.6 us
  Pallas kernels  32.8 us (97%)
  between operations  0.8 us (2%)
    pallas_call x1, Pallas kernels, run_main(): pl.pallas_call(main_kernel, out_shape=outs, in_specs=[pl.BlockSpec(memory...  27.7 us
    pallas_call x1, Pallas kernels, run_weight(): pl.pallas_call(weight_kernel, out_shape=[sds((1, HH, D), f32), sds((1, H)...  5.07 us

profile of v4, /device:TPU:0, one launch (start us, length us, event | category | flops | bytes accessed | tf_op | source)
XLA Modules:
  0.0 33.6 jit_solution(3844179489994602784)
XLA Ops:
  0.6 27.7 %critics.1 = (f32[2048,1024]{1,0:T(8,128)S(1)}, bf16[1024,4096]{1,0:T(8,128)(2,1)S(1)}, bf16[128,1024]{1,0:T(8,128)(2,1)S(1)}, bf16[96,1024]{1,0:T(8,128)(2,1)S(...) custom-call(bf16[256,1024]{1,0:T(8,128)(2,1)} %obs_hbm.1, ...), custom_call_target="tpu_custom_call" | custom-call | tf_op jit(solution)/shard_map/critics/pallas_call | solution.py:441
  28.3 5.1 %weights.1 = (f32[1,2048,1024]{2,1,0:T(8,128)}, f32[1,4096]{1,0:T(1,128)}, f32[1,3]{1,0:T(1,128)}) custom-call(f32[2048,1024]{1,0:T(8,128)S(1)} %get-tuple-element.12.part, bf16[1024,4096]{1,0:T(8,128)(2,1)S(1)} %get-tuple-element.13.wt, bf16[128,1024]{1,0:T(8,128)(2,1)S(1)} %get-tuple-element.14.rt, bf16[96,1024]{1,0:T(8,128)(2,1)S(1)} %get-tuple-element.15.tail_x, ...), custom_call_target="tpu_custom_call" | custom-call | tf_op jit(solution)/shard_map/weights/pallas_call | solution.py:503

commit v5 on v4

--- a/solution.py
+++ b/solution.py
@@ -147,9 +147,10 @@
     obs = dot(rows_oh, tab_obs[...])
     nxt = dot(rows_oh, tab_next[...])
     tx_obs[...] = obs.astype(bf16)
-    half_data = (obs + dot(dact_oh, table[...])).astype(bf16)
+    acts = dot(jnp.concatenate([dact_oh, nact_oh], axis=0), table[...])
+    half_data = (obs + acts[0:S]).astype(bf16)
     xdn[0:S, :] = half_data
-    xdn[S : 2 * S, :] = (nxt + dot(nact_oh, table[...])).astype(bf16)
+    xdn[S : 2 * S, :] = (nxt + acts[S : 2 * S]).astype(bf16)
     xd[0:S, :] = half_data
 
     def own_act(c, q_acc):
@@ -361,13 +362,13 @@
     cp_q_far.wait_recv()
     mass_own, dq_own = penalty(q_own_sc[...] + rx_q_far[...], 0)
     for m in range(nb):
-        if m < 2:
+        if m < 1:
             weight_part(m, 0, False)
         readout_part(m, dq_own, 0, False)
     gw_at = pl.ds(h0, HH)
     cp_gw = far(gw2.at[:, gw_at], gw2.at[:, gw_at], pair_s.at[6], pair_r.at[6], partner)
     cp_gw.start()
-    for m in range(2, nb):
+    for m in range(1, nb):
         weight_part(m, 0, False)
 
     cp_q.wait_recv()

time: 33.7 us -> 33.5 us (level)
  Pallas kernels: 32.8 us -> 32.4 us
    pallas_call x1, Pallas kernels: 27.7 us -> 27.4 us  [run_main(): pl.pallas_call(main_kernel, out_shape=outs, in_specs=[pl.BlockSpec(memory...]
where the time goes in v5:
time: 33.5 us; the launch traced here: 33.2 us
  Pallas kernels  32.4 us (97%)
  between operations  0.8 us (2%)
    pallas_call x1, Pallas kernels, run_main(): pl.pallas_call(main_kernel, out_shape=outs, in_specs=[pl.BlockSpec(memory...  27.4 us
    pallas_call x1, Pallas kernels, run_weight(): pl.pallas_call(weight_kernel, out_shape=[sds((1, HH, D), f32), sds((1, H)...  5.06 us

profile of v5, /device:TPU:0, one launch (start us, length us, event | category | flops | bytes accessed | tf_op | source)
XLA Modules:
  0.0 33.2 jit_solution(10542279085500957927)
XLA Ops:
  0.6 27.4 %critics.1 = (f32[2048,1024]{1,0:T(8,128)S(1)}, bf16[1024,4096]{1,0:T(8,128)(2,1)S(1)}, bf16[128,1024]{1,0:T(8,128)(2,1)S(1)}, bf16[96,1024]{1,0:T(8,128)(2,1)S(...) custom-call(bf16[256,1024]{1,0:T(8,128)(2,1)} %obs_hbm.1, ...), custom_call_target="tpu_custom_call" | custom-call | tf_op jit(solution)/shard_map/critics/pallas_call | solution.py:442
  28.0 5.1 %weights.1 = (f32[1,2048,1024]{2,1,0:T(8,128)}, f32[1,4096]{1,0:T(1,128)}, f32[1,3]{1,0:T(1,128)}) custom-call(f32[2048,1024]{1,0:T(8,128)S(1)} %get-tuple-element.12.part, bf16[1024,4096]{1,0:T(8,128)(2,1)S(1)} %get-tuple-element.13.wt, bf16[128,1024]{1,0:T(8,128)(2,1)S(1)} %get-tuple-element.14.rt, bf16[96,1024]{1,0:T(8,128)(2,1)S(1)} %get-tuple-element.15.tail_x, ...), custom_call_target="tpu_custom_call" | custom-call | tf_op jit(solution)/shard_map/weights/pallas_call | solution.py:504
